TPU v7x, 32 devices: a 4x4x1 block of a 4x4x8 slice. The times are simulated.
32 devices in a mesh: dp: 1 (over z), tp: 4 (over y), cp: 8 (over x, core).
Axes of the slice: x: 4, y: 4, z: 1, core: 2. Of those that a mesh axis runs over, the one named last changes fastest.
The devices are a block of a 4x4x8 slice.
Arguments:
- x: bfloat16 [8192, 3584], P(('dp', 'cp', 'tp'))
- pos: int32 [8192], P(('dp', 'cp', 'tp'))
- g1: bfloat16 [3584], replicated
- g2: bfloat16 [3584], replicated
- wq: bfloat16 [3584, 3584], P(None, 'tp')
- wk: bfloat16 [3584, 512], P(None, 'tp')
- wv: bfloat16 [3584, 512], P(None, 'tp')
- wo: bfloat16 [3584, 3584], P('tp')
- w1: bfloat16 [3584, 18944], P(None, 'tp')
- w3: bfloat16 [3584, 18944], P(None, 'tp')
- w2: bfloat16 [18944, 3584], P('tp')
Outputs:
- output: bfloat16 [8192, 3584], P(('dp', 'cp', 'tp'))
All inputs are finite; a program needn't handle non-finite values.
Results may differ from a plain program's by a relative error of at most 0.00972693.
Values are sent between devices in bfloat16 or wider.
A program may use at most 768 MiB of HBM per device.

v0:
```python
import math
import jax
import jax.numpy as jnp
from jax import lax
from jax.sharding import PartitionSpec as P, NamedSharding

DH = 128
EPS = 1e-5
THETA = 500000.0


def rms_norm(v, g):
    vf = v.astype(jnp.float32)
    inv = lax.rsqrt(jnp.mean(vf * vf, axis=-1, keepdims=True) + EPS)
    return (vf * inv * g.astype(jnp.float32)).astype(jnp.bfloat16)


def rope(y, p):
    half = DH // 2
    freq = 1.0 / (THETA ** (jnp.arange(0, DH, 2, dtype=jnp.float32) / DH))
    ang = p.astype(jnp.float32)[..., None] * freq
    c = jnp.cos(ang)[..., None, :]
    s = jnp.sin(ang)[..., None, :]
    y1 = y[..., :half]
    y2 = y[..., half:]
    return jnp.concatenate([y1 * c - y2 * s, y2 * c + y1 * s], axis=-1)


def attend(q, k, v, qpos, kpos):
    nq, hl, dh = q.shape
    hk = k.shape[1]
    grp = hl // hk
    qb = nq
    while qb % 2 == 0 and qb * hl > 1024:
        qb = qb // 2
    qr = q.reshape(nq // qb, qb, hk, grp, dh)
    pr = qpos.reshape(nq // qb, qb)
    scale = 1.0 / math.sqrt(dh)

    def blk(qp):
        qq, pp = qp
        s = jnp.einsum('qkgd,skd->kgqs', qq, k, preferred_element_type=jnp.float32) * scale
        s = jnp.where(kpos[None, None, None, :] <= pp[None, None, :, None], s, -1e30)
        e = jnp.exp(s - jnp.max(s, axis=-1, keepdims=True))
        w = (e / jnp.sum(e, axis=-1, keepdims=True)).astype(jnp.bfloat16)
        o = jnp.einsum('kgqs,skd->qkgd', w, v, preferred_element_type=jnp.float32)
        return o.astype(jnp.bfloat16)

    return lax.map(blk, (qr, pr)).reshape(nq, hl * dh)


def solution(mesh):
    tok = P(('dp', 'cp', 'tp'), None)
    col = P(None, 'tp')
    row = P('tp', None)

    def local(x, pos, g1, g2, wq, wk, wv, wo, w1, w3, w2):
        a = lax.all_gather(rms_norm(x, g1), 'tp', axis=0, tiled=True)
        pg = lax.all_gather(pos, 'tp', axis=0, tiled=True)
        nr = a.shape[0]
        q = rope(jnp.dot(a, wq, preferred_element_type=jnp.float32).reshape(nr, -1, DH), pg).astype(jnp.bfloat16)
        k = rope(jnp.dot(a, wk, preferred_element_type=jnp.float32).reshape(nr, -1, DH), pg).astype(jnp.bfloat16)
        v = jnp.dot(a, wv, preferred_element_type=jnp.float32).astype(jnp.bfloat16).reshape(nr, -1, DH)
        ka = lax.all_gather(k, 'cp', axis=0, tiled=True)
        va = lax.all_gather(v, 'cp', axis=0, tiled=True)
        pa = lax.all_gather(pg, 'cp', axis=0, tiled=True)
        o = attend(q, ka, va, pg, pa)
        y = lax.psum_scatter(jnp.dot(o, wo, preferred_element_type=jnp.float32), 'tp', scatter_dimension=0, tiled=True)
        h1 = (x.astype(jnp.float32) + y).astype(jnp.bfloat16)
        b = lax.all_gather(rms_norm(h1, g2), 'tp', axis=0, tiled=True)
        hid = (jax.nn.silu(jnp.dot(b, w1, preferred_element_type=jnp.float32)) * jnp.dot(b, w3, preferred_element_type=jnp.float32)).astype(jnp.bfloat16)
        z = lax.psum_scatter(jnp.dot(hid, w2, preferred_element_type=jnp.float32), 'tp', scatter_dimension=0, tiled=True)
        return (h1.astype(jnp.float32) + z).astype(jnp.bfloat16)

    return jax.shard_map(local, mesh=mesh, in_specs=(tok, P(('dp', 'cp', 'tp')), P(None), P(None), col, col, col, row, col, col, row), out_specs=tok, check_vma=False)
```

profile of v0, /device:TPU:97, one launch (start us, length us, event | category | flops | bytes accessed | tf_op | source)
XLA Modules:
  0.0 978.6 jit_solution(2715237325557095292)
XLA Ops:
  6.6 0.8 convert_element_type.69
  7.3 1.9 fusion.30
  9.3 3.2 fusion.32
  12.7 10.5 %all-gather.1 = s32[4,1,256]{2,1,0:T(1,128)S(1)} all-gather(s32[1,1,256]{2,1,0:T(1,128)S(1)} %bitcast.136), channel_id=1, replica_groups=mesh['dp'=1,'tp'=4,'cp'=8] {'tp'}, dimensions={0}, use_global_device_ids=true | all-gather | bytes 5120 | tf_op jit(solution)/shard_map/all_gather | solution.py:59
  23.2 65.3 %all-gather.7.cloned.1.call-done = bf16[1024,3584]{1,0:T(8,128)(2,1)} async-done(((bf16[256,3584]{1,0:T(8,128)(2,1)}), bf16[1024,3584]{1,0:T(8,128)(2,1)}) %all-gather.7.cloned.1.call-update) | async-done | bytes 7340048 | tf_op jit(solution)/shard_map/all_gather | solution.py:58
  88.4 5.6 convolution_bitcast_fusion
  94.1 1.2 fusion.46
  95.2 0.7 pad_maximum_fusion.1
  96.1 5.8 convolution_convert_fusion
  102.1 19.2 %all_gather.19 = s32[8192]{0:T(1024)S(1)} all-gather(s32[1024]{0:T(1024)S(1)} %bitcast.134), channel_id=1, replica_groups=mesh['dp'=1,'tp'=4,'cp'=8] {'cp'}, dimensions={0}, use_global_device_ids=true | all-gather | bytes 36864 | tf_op jit(solution)/shard_map/all_gather | solution.py:66
  121.3 1.0 multiply_cosine_fusion.1
  122.3 11.0 %fusion.51 = f32[1024,896]{0,1:T(8,128)S(1)} fusion(bf16[1024,3584]{1,0:T(8,128)(2,1)} %all-gather.7.cloned.1.call-done, bf16[3584,896]{1,0:T(8,128)(2,1)} %param.17), kind=kOutput, calls=%fused_computation.63 | convolution fusion | flops 6576668672 | bytes 17432576 | tf_op jit(solution)/shard_map/dot_general | solution.py:61
  133.3 0.6 subtract_convert_fusion
  134.0 0.2 copy.19
  134.2 0.2 copy.20
  134.6 2.8 copy.16
  137.4 3.2 copy.17
  140.6 4.4 all-gather.13.cloned.1.call-done
  145.0 331.6 %while.10 = (s32[]{:T(128)}, bf16[8,128,1,7,128]{4,1,3,2,0:T(8,128)(2,1)}, s32[8192]{0:T(1024)S(1)}, s32[8,128]{1,0:T(8,128)S(1)}, bf16[8,128,1,7,128]{4,1,3,2,0...) while((s32[]{:T(128)}, ...), condition=%wide.region_4.5_spmd, body=%wide.region_1.4_spmd.sunk | while | flops 3847338240 | bytes 105369720 | solution.py:49
  145.2 0.6 broadcast_compare_fusion.2
  145.9 13.2 %fusion.82 = (f32[7,128]{1,0:T(8,128)S(1)}, f32[128,7,8192]{2,0,1:T(8,128)}) fusion(pred[128,8192]{1,0:T(8,128)(4,1)S(1)} %broadcast_compare_fusion.2, bf16[8192,1,128]{2,0,1:T(8,128)(2,1)S(1)} %get-tuple-element.156, bf16[8,128,1,7,128]{4,1,3,2,0:T(8,128)(2,1)} %get-tuple-element.155, s32[]{:T(128)} %get-tuple-element.143), kind=kOutput, calls=%fused_computation.4.clone.1 | convolution fusion | flops 1901067392 | bytes 32739328 | tf_op jit(solution)/shard_map/while/body/eval_jaxpr/qkgd,skd->kgqs/dot_general | solution.py:42
  159.0 13.8 %fusion.83 = f32[7,128]{1,0:T(8,128)S(1)} fusion(f32[128,7,8192]{2,0,1:T(8,128)} %get-tuple-element.133, f32[7,128]{1,0:T(8,128)S(1)} %get-tuple-element.134, pred[128,8192]{1,0:T(8,128)(4,1)S(1)} %broadcast_compare_fusion.2), kind=kLoop, calls=%fused_computation.3.clone.1 | loop fusion | flops 29359232 | bytes 30415872 | tf_op jit(solution)/shard_map/while/body/eval_jaxpr/reduce_sum | solution.py:45
  172.9 13.8 %fusion.84 = bf16[8,128,1,7,128]{4,1,3,2,0:T(8,128)(2,1)} fusion(bf16[8,128,1,7,128]{4,1,3,2,0:T(8,128)(2,1)} %get-tuple-element.144, s32[]{:T(128)} %get-tuple-element.143, bf16[8192,1,128]{2,0,1:T(8,128)(2,1)S(1)} %copy-done.8, f32[7,128]{1,0:T(8,128)S(1)} %fusion.83, f32[7,128]{1,0:T(8,128)S(1)} %get-tuple-element.134, ...), kind=kOutput, calls=%fused_computation.13.clone.1 | convolution fusion | flops 1915863040 | bytes 32742912 | tf_op jit(solution)/shard_map/while/body/eval_jaxpr/kgqs,skd->qkgd/dot_general | solution.py:46
  186.6 0.6 broadcast_compare_fusion.2
  187.3 13.2 %fusion.82 = (f32[7,128]{1,0:T(8,128)S(1)}, f32[128,7,8192]{2,0,1:T(8,128)}) fusion(pred[128,8192]{1,0:T(8,128)(4,1)S(1)} %broadcast_compare_fusion.2, bf16[8192,1,128]{2,0,1:T(8,128)(2,1)S(1)} %get-tuple-element.156, bf16[8,128,1,7,128]{4,1,3,2,0:T(8,128)(2,1)} %get-tuple-element.155, s32[]{:T(128)} %get-tuple-element.143), kind=kOutput, calls=%fused_computation.4.clone.1 | convolution fusion | flops 1901067392 | bytes 32739328 | tf_op jit(solution)/shard_map/while/body/eval_jaxpr/qkgd,skd->kgqs/dot_general | solution.py:42
  200.5 13.8 %fusion.83 = f32[7,128]{1,0:T(8,128)S(1)} fusion(f32[128,7,8192]{2,0,1:T(8,128)} %get-tuple-element.133, f32[7,128]{1,0:T(8,128)S(1)} %get-tuple-element.134, pred[128,8192]{1,0:T(8,128)(4,1)S(1)} %broadcast_compare_fusion.2), kind=kLoop, calls=%fused_computation.3.clone.1 | loop fusion | flops 29359232 | bytes 30415872 | tf_op jit(solution)/shard_map/while/body/eval_jaxpr/reduce_sum | solution.py:45
  214.3 13.8 %fusion.84 = bf16[8,128,1,7,128]{4,1,3,2,0:T(8,128)(2,1)} fusion(bf16[8,128,1,7,128]{4,1,3,2,0:T(8,128)(2,1)} %get-tuple-element.144, s32[]{:T(128)} %get-tuple-element.143, bf16[8192,1,128]{2,0,1:T(8,128)(2,1)S(1)} %copy-done.8, f32[7,128]{1,0:T(8,128)S(1)} %fusion.83, f32[7,128]{1,0:T(8,128)S(1)} %get-tuple-element.134, ...), kind=kOutput, calls=%fused_computation.13.clone.1 | convolution fusion | flops 1915863040 | bytes 32742912 | tf_op jit(solution)/shard_map/while/body/eval_jaxpr/kgqs,skd->qkgd/dot_general | solution.py:46
  228.1 0.6 broadcast_compare_fusion.2
  228.7 13.2 %fusion.82 = (f32[7,128]{1,0:T(8,128)S(1)}, f32[128,7,8192]{2,0,1:T(8,128)}) fusion(pred[128,8192]{1,0:T(8,128)(4,1)S(1)} %broadcast_compare_fusion.2, bf16[8192,1,128]{2,0,1:T(8,128)(2,1)S(1)} %get-tuple-element.156, bf16[8,128,1,7,128]{4,1,3,2,0:T(8,128)(2,1)} %get-tuple-element.155, s32[]{:T(128)} %get-tuple-element.143), kind=kOutput, calls=%fused_computation.4.clone.1 | convolution fusion | flops 1901067392 | bytes 32739328 | tf_op jit(solution)/shard_map/while/body/eval_jaxpr/qkgd,skd->kgqs/dot_general | solution.py:42
  241.9 13.8 %fusion.83 = f32[7,128]{1,0:T(8,128)S(1)} fusion(f32[128,7,8192]{2,0,1:T(8,128)} %get-tuple-element.133, f32[7,128]{1,0:T(8,128)S(1)} %get-tuple-element.134, pred[128,8192]{1,0:T(8,128)(4,1)S(1)} %broadcast_compare_fusion.2), kind=kLoop, calls=%fused_computation.3.clone.1 | loop fusion | flops 29359232 | bytes 30415872 | tf_op jit(solution)/shard_map/while/body/eval_jaxpr/reduce_sum | solution.py:45
  255.7 13.8 %fusion.84 = bf16[8,128,1,7,128]{4,1,3,2,0:T(8,128)(2,1)} fusion(bf16[8,128,1,7,128]{4,1,3,2,0:T(8,128)(2,1)} %get-tuple-element.144, s32[]{:T(128)} %get-tuple-element.143, bf16[8192,1,128]{2,0,1:T(8,128)(2,1)S(1)} %copy-done.8, f32[7,128]{1,0:T(8,128)S(1)} %fusion.83, f32[7,128]{1,0:T(8,128)S(1)} %get-tuple-element.134, ...), kind=kOutput, calls=%fused_computation.13.clone.1 | convolution fusion | flops 1915863040 | bytes 32742912 | tf_op jit(solution)/shard_map/while/body/eval_jaxpr/kgqs,skd->qkgd/dot_general | solution.py:46
  269.5 0.6 broadcast_compare_fusion.2
  270.1 13.2 %fusion.82 = (f32[7,128]{1,0:T(8,128)S(1)}, f32[128,7,8192]{2,0,1:T(8,128)}) fusion(pred[128,8192]{1,0:T(8,128)(4,1)S(1)} %broadcast_compare_fusion.2, bf16[8192,1,128]{2,0,1:T(8,128)(2,1)S(1)} %get-tuple-element.156, bf16[8,128,1,7,128]{4,1,3,2,0:T(8,128)(2,1)} %get-tuple-element.155, s32[]{:T(128)} %get-tuple-element.143), kind=kOutput, calls=%fused_computation.4.clone.1 | convolution fusion | flops 1901067392 | bytes 32739328 | tf_op jit(solution)/shard_map/while/body/eval_jaxpr/qkgd,skd->kgqs/dot_general | solution.py:42
  283.3 13.8 %fusion.83 = f32[7,128]{1,0:T(8,128)S(1)} fusion(f32[128,7,8192]{2,0,1:T(8,128)} %get-tuple-element.133, f32[7,128]{1,0:T(8,128)S(1)} %get-tuple-element.134, pred[128,8192]{1,0:T(8,128)(4,1)S(1)} %broadcast_compare_fusion.2), kind=kLoop, calls=%fused_computation.3.clone.1 | loop fusion | flops 29359232 | bytes 30415872 | tf_op jit(solution)/shard_map/while/body/eval_jaxpr/reduce_sum | solution.py:45
  297.1 13.8 %fusion.84 = bf16[8,128,1,7,128]{4,1,3,2,0:T(8,128)(2,1)} fusion(bf16[8,128,1,7,128]{4,1,3,2,0:T(8,128)(2,1)} %get-tuple-element.144, s32[]{:T(128)} %get-tuple-element.143, bf16[8192,1,128]{2,0,1:T(8,128)(2,1)S(1)} %copy-done.8, f32[7,128]{1,0:T(8,128)S(1)} %fusion.83, f32[7,128]{1,0:T(8,128)S(1)} %get-tuple-element.134, ...), kind=kOutput, calls=%fused_computation.13.clone.1 | convolution fusion | flops 1915863040 | bytes 32742912 | tf_op jit(solution)/shard_map/while/body/eval_jaxpr/kgqs,skd->qkgd/dot_general | solution.py:46
  310.9 0.6 broadcast_compare_fusion.2
  311.6 13.2 %fusion.82 = (f32[7,128]{1,0:T(8,128)S(1)}, f32[128,7,8192]{2,0,1:T(8,128)}) fusion(pred[128,8192]{1,0:T(8,128)(4,1)S(1)} %broadcast_compare_fusion.2, bf16[8192,1,128]{2,0,1:T(8,128)(2,1)S(1)} %get-tuple-element.156, bf16[8,128,1,7,128]{4,1,3,2,0:T(8,128)(2,1)} %get-tuple-element.155, s32[]{:T(128)} %get-tuple-element.143), kind=kOutput, calls=%fused_computation.4.clone.1 | convolution fusion | flops 1901067392 | bytes 32739328 | tf_op jit(solution)/shard_map/while/body/eval_jaxpr/qkgd,skd->kgqs/dot_general | solution.py:42
  324.7 13.8 %fusion.83 = f32[7,128]{1,0:T(8,128)S(1)} fusion(f32[128,7,8192]{2,0,1:T(8,128)} %get-tuple-element.133, f32[7,128]{1,0:T(8,128)S(1)} %get-tuple-element.134, pred[128,8192]{1,0:T(8,128)(4,1)S(1)} %broadcast_compare_fusion.2), kind=kLoop, calls=%fused_computation.3.clone.1 | loop fusion | flops 29359232 | bytes 30415872 | tf_op jit(solution)/shard_map/while/body/eval_jaxpr/reduce_sum | solution.py:45
  338.5 13.8 %fusion.84 = bf16[8,128,1,7,128]{4,1,3,2,0:T(8,128)(2,1)} fusion(bf16[8,128,1,7,128]{4,1,3,2,0:T(8,128)(2,1)} %get-tuple-element.144, s32[]{:T(128)} %get-tuple-element.143, bf16[8192,1,128]{2,0,1:T(8,128)(2,1)S(1)} %copy-done.8, f32[7,128]{1,0:T(8,128)S(1)} %fusion.83, f32[7,128]{1,0:T(8,128)S(1)} %get-tuple-element.134, ...), kind=kOutput, calls=%fused_computation.13.clone.1 | convolution fusion | flops 1915863040 | bytes 32742912 | tf_op jit(solution)/shard_map/while/body/eval_jaxpr/kgqs,skd->qkgd/dot_general | solution.py:46
  352.3 0.6 broadcast_compare_fusion.2
  353.0 13.2 %fusion.82 = (f32[7,128]{1,0:T(8,128)S(1)}, f32[128,7,8192]{2,0,1:T(8,128)}) fusion(pred[128,8192]{1,0:T(8,128)(4,1)S(1)} %broadcast_compare_fusion.2, bf16[8192,1,128]{2,0,1:T(8,128)(2,1)S(1)} %get-tuple-element.156, bf16[8,128,1,7,128]{4,1,3,2,0:T(8,128)(2,1)} %get-tuple-element.155, s32[]{:T(128)} %get-tuple-element.143), kind=kOutput, calls=%fused_computation.4.clone.1 | convolution fusion | flops 1901067392 | bytes 32739328 | tf_op jit(solution)/shard_map/while/body/eval_jaxpr/qkgd,skd->kgqs/dot_general | solution.py:42
  366.2 13.8 %fusion.83 = f32[7,128]{1,0:T(8,128)S(1)} fusion(f32[128,7,8192]{2,0,1:T(8,128)} %get-tuple-element.133, f32[7,128]{1,0:T(8,128)S(1)} %get-tuple-element.134, pred[128,8192]{1,0:T(8,128)(4,1)S(1)} %broadcast_compare_fusion.2), kind=kLoop, calls=%fused_computation.3.clone.1 | loop fusion | flops 29359232 | bytes 30415872 | tf_op jit(solution)/shard_map/while/body/eval_jaxpr/reduce_sum | solution.py:45
  380.0 13.8 %fusion.84 = bf16[8,128,1,7,128]{4,1,3,2,0:T(8,128)(2,1)} fusion(bf16[8,128,1,7,128]{4,1,3,2,0:T(8,128)(2,1)} %get-tuple-element.144, s32[]{:T(128)} %get-tuple-element.143, bf16[8192,1,128]{2,0,1:T(8,128)(2,1)S(1)} %copy-done.8, f32[7,128]{1,0:T(8,128)S(1)} %fusion.83, f32[7,128]{1,0:T(8,128)S(1)} %get-tuple-element.134, ...), kind=kOutput, calls=%fused_computation.13.clone.1 | convolution fusion | flops 1915863040 | bytes 32742912 | tf_op jit(solution)/shard_map/while/body/eval_jaxpr/kgqs,skd->qkgd/dot_general | solution.py:46
  393.8 0.6 broadcast_compare_fusion.2
  394.4 13.2 %fusion.82 = (f32[7,128]{1,0:T(8,128)S(1)}, f32[128,7,8192]{2,0,1:T(8,128)}) fusion(pred[128,8192]{1,0:T(8,128)(4,1)S(1)} %broadcast_compare_fusion.2, bf16[8192,1,128]{2,0,1:T(8,128)(2,1)S(1)} %get-tuple-element.156, bf16[8,128,1,7,128]{4,1,3,2,0:T(8,128)(2,1)} %get-tuple-element.155, s32[]{:T(128)} %get-tuple-element.143), kind=kOutput, calls=%fused_computation.4.clone.1 | convolution fusion | flops 1901067392 | bytes 32739328 | tf_op jit(solution)/shard_map/while/body/eval_jaxpr/qkgd,skd->kgqs/dot_general | solution.py:42
  407.6 13.8 %fusion.83 = f32[7,128]{1,0:T(8,128)S(1)} fusion(f32[128,7,8192]{2,0,1:T(8,128)} %get-tuple-element.133, f32[7,128]{1,0:T(8,128)S(1)} %get-tuple-element.134, pred[128,8192]{1,0:T(8,128)(4,1)S(1)} %broadcast_compare_fusion.2), kind=kLoop, calls=%fused_computation.3.clone.1 | loop fusion | flops 29359232 | bytes 30415872 | tf_op jit(solution)/shard_map/while/body/eval_jaxpr/reduce_sum | solution.py:45
  421.4 13.8 %fusion.84 = bf16[8,128,1,7,128]{4,1,3,2,0:T(8,128)(2,1)} fusion(bf16[8,128,1,7,128]{4,1,3,2,0:T(8,128)(2,1)} %get-tuple-element.144, s32[]{:T(128)} %get-tuple-element.143, bf16[8192,1,128]{2,0,1:T(8,128)(2,1)S(1)} %copy-done.8, f32[7,128]{1,0:T(8,128)S(1)} %fusion.83, f32[7,128]{1,0:T(8,128)S(1)} %get-tuple-element.134, ...), kind=kOutput, calls=%fused_computation.13.clone.1 | convolution fusion | flops 1915863040 | bytes 32742912 | tf_op jit(solution)/shard_map/while/body/eval_jaxpr/kgqs,skd->qkgd/dot_general | solution.py:46
  435.2 0.6 broadcast_compare_fusion.2
  435.8 13.2 %fusion.82 = (f32[7,128]{1,0:T(8,128)S(1)}, f32[128,7,8192]{2,0,1:T(8,128)}) fusion(pred[128,8192]{1,0:T(8,128)(4,1)S(1)} %broadcast_compare_fusion.2, bf16[8192,1,128]{2,0,1:T(8,128)(2,1)S(1)} %get-tuple-element.156, bf16[8,128,1,7,128]{4,1,3,2,0:T(8,128)(2,1)} %get-tuple-element.155, s32[]{:T(128)} %get-tuple-element.143), kind=kOutput, calls=%fused_computation.4.clone.1 | convolution fusion | flops 1901067392 | bytes 32739328 | tf_op jit(solution)/shard_map/while/body/eval_jaxpr/qkgd,skd->kgqs/dot_general | solution.py:42
  449.0 13.8 %fusion.83 = f32[7,128]{1,0:T(8,128)S(1)} fusion(f32[128,7,8192]{2,0,1:T(8,128)} %get-tuple-element.133, f32[7,128]{1,0:T(8,128)S(1)} %get-tuple-element.134, pred[128,8192]{1,0:T(8,128)(4,1)S(1)} %broadcast_compare_fusion.2), kind=kLoop, calls=%fused_computation.3.clone.1 | loop fusion | flops 29359232 | bytes 30415872 | tf_op jit(solution)/shard_map/while/body/eval_jaxpr/reduce_sum | solution.py:45
  462.8 13.8 %fusion.84 = bf16[8,128,1,7,128]{4,1,3,2,0:T(8,128)(2,1)} fusion(bf16[8,128,1,7,128]{4,1,3,2,0:T(8,128)(2,1)} %get-tuple-element.144, s32[]{:T(128)} %get-tuple-element.143, bf16[8192,1,128]{2,0,1:T(8,128)(2,1)S(1)} %copy-done.8, f32[7,128]{1,0:T(8,128)S(1)} %fusion.83, f32[7,128]{1,0:T(8,128)S(1)} %get-tuple-element.134, ...), kind=kOutput, calls=%fused_computation.13.clone.1 | convolution fusion | flops 1915863040 | bytes 32742912 | tf_op jit(solution)/shard_map/while/body/eval_jaxpr/kgqs,skd->qkgd/dot_general | solution.py:46
  476.6 3.1 copy.18
  479.7 13.9 %fusion.38 = f32[1024,3584]{1,0:T(8,128)} fusion(bf16[896,3584]{1,0:T(8,128)(2,1)} %param.20, bf16[112,8,8,128]{3,2,1,0:T(8,128)(2,1)S(1)} %bitcast.132), kind=kOutput, calls=%fused_computation.38 | convolution fusion | flops 6576668672 | bytes 22937600 | tf_op jit(solution)/shard_map/dot_general | solution.py:68
  493.8 0.6 copy-done.5
  494.3 128.5 %reduce-scatter.3.cloned.1.call-done = f32[256,3584]{1,0:T(8,128)} async-done(((f32[1024,3584]{1,0:T(8,128)}), f32[256,3584]{1,0:T(8,128)}) %reduce-scatter.3.cloned.1.call-update) | async-done | bytes 3670032 | tf_op jit(solution)/shard_map/reduce_scatter | solution.py:68
  622.9 2.7 fusion.34
  625.6 1.3 copy-done.2
  626.8 1.7 fusion.36
  628.7 71.7 %all-gather.11.cloned.1.call-done = bf16[1024,3584]{1,0:T(8,128)(2,1)} async-done(((bf16[256,3584]{1,0:T(8,128)(2,1)}), bf16[1024,3584]{1,0:T(8,128)(2,1)}) %all-gather.11.cloned.1.call-update) | async-done | bytes 7340048 | tf_op jit(solution)/shard_map/all_gather | solution.py:70
  700.5 47.8 %fusion.52 = f32[1024,4736]{1,0:T(8,128)} fusion(bf16[1024,3584]{1,0:T(8,128)(2,1)} %all-gather.11.cloned.1.call-done, bf16[3584,4736]{1,0:T(8,128)(2,1)} %param.21), kind=kOutput, calls=%fused_computation.64 | convolution fusion | flops 34762391552 | bytes 60686336 | tf_op jit(solution)/shard_map/dot_general | solution.py:71
  748.3 45.6 %multiply_convert_fusion.clone.4 = bf16[1024,4736]{1,0:T(8,128)(2,1)} fusion(f32[1024,4736]{1,0:T(8,128)} %fusion.52, bf16[1024,3584]{1,0:T(8,128)(2,1)S(1)} %copy-done.7, bf16[3584,4736]{1,0:T(8,128)(2,1)} %param.22), kind=kOutput, calls=%fused_computation.21.clone.clone.clone.1 | convolution fusion | flops 34791489536 | bytes 70385664 | tf_op jit(solution)/shard_map/dot_general | solution.py:71
  793.9 43.7 %fusion.28 = f32[1024,3584]{1,0:T(8,128)} fusion(bf16[4736,3584]{1,0:T(8,128)(2,1)} %param.23, bf16[1024,4736]{1,0:T(8,128)(2,1)} %multiply_convert_fusion.clone.4), kind=kOutput, calls=%fused_computation.22 | convolution fusion | flops 34762391552 | bytes 58327040 | tf_op jit(solution)/shard_map/dot_general | solution.py:72
  837.7 129.9 %reduce-scatter.5.cloned.1.call-done = f32[256,3584]{1,0:T(8,128)} async-done(((f32[1024,3584]{1,0:T(8,128)}), f32[256,3584]{1,0:T(8,128)}) %reduce-scatter.5.cloned.1.call-update) | async-done | bytes 3670032 | tf_op jit(solution)/shard_map/reduce_scatter | solution.py:72
  967.6 3.7 fusion.37
  (60 shorter events, 1.0 us)
Async XLA Ops:
  6.5 81.9 %copy-start = (bf16[3584,128]{1,0:T(8,128)(2,1)S(1)}, bf16[3584,128]{1,0:T(8,128)(2,1)}, u32[]{:S(2)}) copy-start(bf16[3584,128]{1,0:T(8,128)(2,1)} %param.18) | copy-start | bytes 2752516
  6.6 6.1 copy-start.6
  6.6 81.9 %all-gather.7.cloned.1.call-start = ((), (), s32[]{:S(2)}) async-start(), calls=%async_computation.2 | async-start | bytes 9175040 | tf_op jit(solution)/shard_map/all_gather | solution.py:58
  12.6 124.8 %all-gather.9.cloned.1.call-start = ((), (), s32[]{:S(2)}) async-start(), calls=%async_computation.3 | async-start | bytes 2359296 | tf_op jit(solution)/shard_map/all_gather | solution.py:64
  23.2 72.9 %copy-start.9 = (bf16[3584,128]{1,0:T(8,128)(2,1)S(1)}, bf16[3584,128]{1,0:T(8,128)(2,1)}, u32[]{:S(2)}) copy-start(bf16[3584,128]{1,0:T(8,128)(2,1)} %param.19) | copy-start | bytes 2752516
  96.0 49.0 %all-gather.13.cloned.1.call-start = ((), (), s32[]{:S(2)}) async-start(), calls=%async_computation.7 | async-start | bytes 2359296 | tf_op jit(solution)/shard_map/all_gather | solution.py:65
  102.0 520.9 %reduce-scatter.3.cloned.1.call-start = ((), (), s32[]{:S(2)}) async-start(), calls=%async_computation.4 | async-start | bytes 18350080 | tf_op jit(solution)/shard_map/reduce_scatter | solution.py:68
  159.0 13.8 %copy-start.8 = (bf16[8192,1,128]{2,0,1:T(8,128)(2,1)S(1)}, bf16[8192,1,128]{2,0,1:T(8,128)(2,1)}, u32[]{:S(2)}) copy-start(bf16[8192,1,128]{2,0,1:T(8,128)(2,1)} %get-tuple-element.157) | copy-start | bytes 6291460 | tf_op jit(solution)/shard_map/while
  200.5 13.8 %copy-start.8 = (bf16[8192,1,128]{2,0,1:T(8,128)(2,1)S(1)}, bf16[8192,1,128]{2,0,1:T(8,128)(2,1)}, u32[]{:S(2)}) copy-start(bf16[8192,1,128]{2,0,1:T(8,128)(2,1)} %get-tuple-element.157) | copy-start | bytes 6291460 | tf_op jit(solution)/shard_map/while
  241.9 13.8 %copy-start.8 = (bf16[8192,1,128]{2,0,1:T(8,128)(2,1)S(1)}, bf16[8192,1,128]{2,0,1:T(8,128)(2,1)}, u32[]{:S(2)}) copy-start(bf16[8192,1,128]{2,0,1:T(8,128)(2,1)} %get-tuple-element.157) | copy-start | bytes 6291460 | tf_op jit(solution)/shard_map/while
  283.3 13.8 %copy-start.8 = (bf16[8192,1,128]{2,0,1:T(8,128)(2,1)S(1)}, bf16[8192,1,128]{2,0,1:T(8,128)(2,1)}, u32[]{:S(2)}) copy-start(bf16[8192,1,128]{2,0,1:T(8,128)(2,1)} %get-tuple-element.157) | copy-start | bytes 6291460 | tf_op jit(solution)/shard_map/while
  324.7 13.8 %copy-start.8 = (bf16[8192,1,128]{2,0,1:T(8,128)(2,1)S(1)}, bf16[8192,1,128]{2,0,1:T(8,128)(2,1)}, u32[]{:S(2)}) copy-start(bf16[8192,1,128]{2,0,1:T(8,128)(2,1)} %get-tuple-element.157) | copy-start | bytes 6291460 | tf_op jit(solution)/shard_map/while
  366.1 13.8 %copy-start.8 = (bf16[8192,1,128]{2,0,1:T(8,128)(2,1)S(1)}, bf16[8192,1,128]{2,0,1:T(8,128)(2,1)}, u32[]{:S(2)}) copy-start(bf16[8192,1,128]{2,0,1:T(8,128)(2,1)} %get-tuple-element.157) | copy-start | bytes 6291460 | tf_op jit(solution)/shard_map/while
  407.6 13.8 %copy-start.8 = (bf16[8192,1,128]{2,0,1:T(8,128)(2,1)S(1)}, bf16[8192,1,128]{2,0,1:T(8,128)(2,1)}, u32[]{:S(2)}) copy-start(bf16[8192,1,128]{2,0,1:T(8,128)(2,1)} %get-tuple-element.157) | copy-start | bytes 6291460 | tf_op jit(solution)/shard_map/while
  449.0 13.8 %copy-start.8 = (bf16[8192,1,128]{2,0,1:T(8,128)(2,1)S(1)}, bf16[8192,1,128]{2,0,1:T(8,128)(2,1)}, u32[]{:S(2)}) copy-start(bf16[8192,1,128]{2,0,1:T(8,128)(2,1)} %get-tuple-element.157) | copy-start | bytes 6291460 | tf_op jit(solution)/shard_map/while
  493.6 0.7 copy-start.5
  493.6 129.2 %copy-start.4 = (bf16[256,3584]{1,0:T(8,128)(2,1)S(1)}, bf16[256,3584]{1,0:T(8,128)(2,1)}, u32[]{:S(2)}) copy-start(bf16[256,3584]{1,0:T(8,128)(2,1)} %param.13) | copy-start | bytes 5505028
  493.7 206.8 %all-gather.11.cloned.1.call-start = ((), (), s32[]{:S(2)}) async-start(), calls=%async_computation.5 | async-start | bytes 9175040 | tf_op jit(solution)/shard_map/all_gather | solution.py:70
  625.6 1.3 copy-start.2
  628.6 339.0 %reduce-scatter.5.cloned.1.call-start = ((), (), s32[]{:S(2)}) async-start(), calls=%async_computation.6 | async-start | bytes 18350080 | tf_op jit(solution)/shard_map/reduce_scatter | solution.py:72
  700.5 47.8 %copy-start.7 = (bf16[1024,3584]{1,0:T(8,128)(2,1)S(1)}, bf16[1024,3584]{1,0:T(8,128)(2,1)}, u32[]{:S(2)}) copy-start(bf16[1024,3584]{1,0:T(8,128)(2,1)} %all-gather.11.cloned.1.call-done) | copy-start | bytes 22020100
  837.6 130.0 %copy-start.3 = (bf16[256,3584]{1,0:T(8,128)(2,1)S(1)}, bf16[256,3584]{1,0:T(8,128)(2,1)}, u32[]{:S(2)}) copy-start(bf16[256,3584]{1,0:T(8,128)(2,1)} %copy-done.2) | copy-start | bytes 5505028
  837.7 133.6 %copy-start.1 = (bf16[3584,128]{1,0:T(8,128)(2,1)S(1)}, bf16[3584,128]{1,0:T(8,128)(2,1)}, u32[]{:S(2)}) copy-start(bf16[3584,128]{1,0:T(8,128)(2,1)} %param.18) | copy-start | bytes 2752516
Sparse Core Ops, SparseCore 0:
  12.7 75.6 all-gather.6
  96.1 24.2 all-gather.8
  122.0 22.9 all-gather.12
  493.8 129.0 reduce-scatter.2
  628.8 71.6 all-gather.10
  837.8 129.7 reduce-scatter.4
where the time goes:
time: 984 us; the launch traced here: 979 us
  waiting for transfers between devices  400 us (41%)
  matrix products  389 us (40%)
  other arithmetic  133 us (14%)
  blocking collectives  29.7 us (3%)
  between operations  14.1 us (1%)
  local copies, waits for them, and re-layouts  11.4 us (1%)
    reduce_scatter x1, waiting for transfers between devices, local(): lax.psum_scatter(jnp.dot(hid, w2, preferred_element_type=jnp.float32), 't...  130 us
    reduce_scatter x1, waiting for transfers between devices, local(): lax.psum_scatter(jnp.dot(o, wo, preferred_element_type=jnp.float32), 'tp'...  129 us
    reduce_sum x8, other arithmetic, blk(): w = (e / jnp.sum(e, axis=-1, keepdims=True)).astype(jnp.bfloat16)  110 us
    dot_general x8, matrix products, blk(): o = jnp.einsum('kgqs,skd->qkgd', w, v, preferred_element_type=jnp.float32)  110 us
    dot_general x8, matrix products, blk(): jnp.einsum('qkgd,skd->kgqs', qq, k, preferred_element_type=jnp.float32)  105 us
    all_gather x1, waiting for transfers between devices, local(): b = lax.all_gather(rms_norm(h1, g2), 'tp', axis=0, tiled=True)  71.7 us
    all_gather x1, waiting for transfers between devices, local(): a = lax.all_gather(rms_norm(x, g1), 'tp', axis=0, tiled=True)  65.3 us
    dot_general x1, matrix products, local(): jnp.dot(b, w1, preferred_element_type=jnp.float32)  47.8 us
  transfers between devices with their start and end apart: 6, of which 5 were waited for; matrix products, arithmetic and copies ran while one was open for 3% of the time, Pallas kernels for 0%

commit v1 on v0

v1 whole, which is shorter than its diff:
```python
import functools
import math
import jax
import jax.numpy as jnp
from jax import lax
from jax.experimental import pallas as pl
from jax.experimental.pallas import tpu as pltpu
from jax.sharding import PartitionSpec as P

DH = 128
EPS = 1e-5
THETA = 500000.0
NEG = -1e30


def rms_norm(v, g):
    vf = v.astype(jnp.float32)
    inv = lax.rsqrt(jnp.mean(vf * vf, axis=-1, keepdims=True) + EPS)
    return (vf * inv * g.astype(jnp.float32)).astype(jnp.bfloat16)


def rope(y, p):
    half = DH // 2
    freq = 1.0 / (THETA ** (jnp.arange(0, DH, 2, dtype=jnp.float32) / DH))
    ang = p.astype(jnp.float32)[..., None] * freq
    c = jnp.cos(ang)[..., None, :]
    s = jnp.sin(ang)[..., None, :]
    y1 = y[..., :half]
    y2 = y[..., half:]
    return jnp.concatenate([y1 * c - y2 * s, y2 * c + y1 * s], axis=-1)


def attn_body(rev, npiece, nblk, c_ref, q_ref, *refs):
    if rev:
        kva_ref, kvb_ref, o_ref, acc, m_s, l_s = refs
    else:
        kva_ref, o_ref, acc, m_s, l_s = refs
    c = c_ref[0]
    n = q_ref.shape[0]
    bk = n
    coef = math.log2(math.e) / math.sqrt(DH)
    q = q_ref[...]

    def step(kv_ref, i, diag, first):
        k = kv_ref[pl.ds(i * bk, bk), :DH]
        v = kv_ref[pl.ds(i * bk, bk), DH:]
        s = lax.dot_general(q, k, (((1,), (1,)), ((), ())), preferred_element_type=jnp.float32)
        if diag:
            r = lax.broadcasted_iota(jnp.int32, (n, bk), 0)
            t = lax.broadcasted_iota(jnp.int32, (n, bk), 1)
            if rev:
                piece = n // npiece
                r = (npiece - 1 - r // piece) * piece + r % piece
                t = (npiece - 1 - t // piece) * piece + t % piece
            s = jnp.where(t <= r, s, NEG)
        mx = jnp.max(s, axis=1, keepdims=True)
        if first:
            m = mx
        else:
            m0 = m_s[:, :1]
            m = jnp.maximum(m0, mx)
        p = jnp.exp2((s - m) * coef)
        part = p[:, :128]
        for u in range(1, bk // 128):
            part = part + p[:, u * 128:(u + 1) * 128]
        pv = jnp.dot(p.astype(jnp.bfloat16), v, preferred_element_type=jnp.float32)
        if first:
            l_s[...] = part
            acc[...] = pv
        else:
            al = jnp.exp2((m0 - m) * coef)
            l_s[...] = l_s[...] * al + part
            acc[...] = acc[...] * al + pv
        m_s[...] = jnp.broadcast_to(m, m_s.shape)

    step(kvb_ref if rev else kva_ref, c, True, True)
    if rev:
        @pl.loop(0, nblk)
        def _(i):
            step(kva_ref, i, False, False)

        @pl.loop(c + 1, nblk)
        def _(i):
            step(kvb_ref, i, False, False)
    else:
        @pl.loop(0, c)
        def _(i):
            step(kva_ref, i, False, False)
    l = jnp.sum(l_s[...], axis=1, keepdims=True)
    o_ref[...] = (acc[...] / l).astype(o_ref.dtype)


def attend(rev, npiece, nblk, c, q, *kvs):
    n, w = q.shape
    heads = w // DH
    units = (nblk + 1 + nblk // 2) if rev else nblk // 2 + 1
    gs = pltpu.PrefetchScalarGridSpec(
        num_scalar_prefetch=1,
        grid=(heads,),
        in_specs=[pl.BlockSpec((n, DH), lambda h, c: (0, h))]
        + [pl.BlockSpec(kv.shape, lambda h, c: (0, 0)) for kv in kvs],
        out_specs=pl.BlockSpec((n, DH), lambda h, c: (0, h)),
        scratch_shapes=[pltpu.VMEM((n, DH), jnp.float32)] * 3,
    )
    return pl.pallas_call(
        functools.partial(attn_body, rev, npiece, nblk),
        grid_spec=gs,
        out_shape=jax.ShapeDtypeStruct((n, w), jnp.bfloat16),
        compiler_params=pltpu.CompilerParams(dimension_semantics=("arbitrary",)),
        cost_estimate=pl.CostEstimate(
            flops=units * heads * n * n * DH * 4 * 3, bytes_accessed=3 * n * w * 2 + sum(kv.size * 2 for kv in kvs),
            transcendentals=units * heads * n * n),
        name="attn_b" if rev else "attn_a",
    )(c, q, *kvs)


def solution(mesh):
    tok = P(('dp', 'cp', 'tp'), None)
    col = P(None, 'tp')
    row = P('tp', None)
    ntp = mesh.shape['tp']
    ncp = mesh.shape['cp']

    def local(x, pos, g1, g2, wq, wk, wv, wo, w1, w3, w2):
        f32 = jnp.float32
        half = x.shape[0] // 2
        xs = [x[:half], x[half:]]
        pg = lax.all_gather(pos, 'tp', axis=0).reshape(ntp, 2, half)
        cidx = lax.axis_index('cp').astype(jnp.int32).reshape(1)
        ag = lambda u: lax.all_gather(u, 'tp', axis=0, tiled=True)
        dot = lambda u, w: jnp.dot(u, w, preferred_element_type=f32)

        an0 = rms_norm(xs[0], g1)
        an0, xb = lax.optimization_barrier((an0, xs[1]))
        ans = [an0, rms_norm(xb, g1)]
        qs, kvs = [], []
        for i in range(2):
            a = ag(ans[i])
            p = pg[:, i].reshape(-1)
            nr = a.shape[0]
            k = rope(dot(a, wk).reshape(nr, -1, DH), p).astype(jnp.bfloat16).reshape(nr, -1)
            v = dot(a, wv).astype(jnp.bfloat16)
            kvs.append(lax.all_gather(jnp.concatenate([k, v], axis=1), 'cp', axis=0, tiled=True))
            qs.append(rope(dot(a, wq).reshape(nr, -1, DH), p).astype(jnp.bfloat16).reshape(nr, -1))

        outs = []
        oa = attend(False, ntp, ncp, cidx, qs[0], kvs[0])
        oa, qb = lax.optimization_barrier((oa, qs[1]))
        ya = dot(oa, wo).astype(jnp.bfloat16)
        ya, qb = lax.optimization_barrier((ya, qb))
        os = [oa, attend(True, ntp, ncp, cidx, qb, kvs[0], kvs[1])]
        bn = None
        for i in range(2):
            y = ya if i == 0 else dot(os[i], wo).astype(jnp.bfloat16)
            y = lax.psum_scatter(y, 'tp', scatter_dimension=0, tiled=True)
            if bn is not None:
                y, bn = lax.optimization_barrier((y, bn))
            h1 = (xs[i].astype(f32) + y.astype(f32)).astype(jnp.bfloat16)
            bn = rms_norm(h1, g2)
            b = ag(bn)
            hid = (jax.nn.silu(dot(b, w1)) * dot(b, w3)).astype(jnp.bfloat16)
            z = lax.psum_scatter(dot(hid, w2).astype(jnp.bfloat16), 'tp', scatter_dimension=0, tiled=True)
            outs.append((h1.astype(f32) + z.astype(f32)).astype(jnp.bfloat16))
        return jnp.concatenate(outs, axis=0)

    return jax.shard_map(local, mesh=mesh, in_specs=(tok, P(('dp', 'cp', 'tp')), P(None), P(None), col, col, col, row, col, col, row), out_specs=tok, check_vma=False)
```

time: 984 us -> 590 us (0.60)
  waiting for transfers between devices: 400 us -> 197 us
  matrix products: 389 us -> 209 us
  Pallas kernels: 0 us -> 124 us
  other arithmetic: 133 us -> 23.9 us
  blocking collectives: 29.7 us -> 10.5 us
    dot_general x23 -> x14, matrix products: 389 us -> 209 us  [local(): dot = lambda u, w: jnp.dot(u, w, preferred_element_type=f32)]
    reduce_scatter x2 -> x4, waiting for transfers between devices: 258 us -> 79.2 us  [the longest x2 40.5 us: local(): lax.psum_scatter(dot(hid, w2).astype(jnp.bfloat16), 'tp', scatter_dimensi...]
    pallas_call x0 -> x2, Pallas kernels: none -> 124 us  [attend(): pl.pallas_call(functools.partial(attn_body, rev, npiece, nblk), grid_spec...]
    reduce_sum x8 -> x0, other arithmetic: 110 us -> none  [blk(): w = (e / jnp.sum(e, axis=-1, keepdims=True)).astype(jnp.bfloat16)]
    all_gather x4 -> x6, waiting for transfers between devices: 141 us -> 116 us  [the longest x4 113 us: local(): ag = lambda u: lax.all_gather(u, 'tp', axis=0, tiled=True)]
    all_gather x2 -> x1, blocking collectives: 29.7 us -> 10.5 us  [local(): pg = lax.all_gather(pos, 'tp', axis=0).reshape(ntp, 2, half)]
  transfers between devices with their start and end apart: 6 -> 10, of which waited for: 5 -> 6; matrix products, arithmetic and copies ran while one was open for 3% -> 37% of each run, Pallas kernels for 0% -> 21%
where the time goes in v1:
time: 590 us; the launch traced here: 585 us
  matrix products  209 us (35%)
  waiting for transfers between devices  197 us (33%)
  Pallas kernels  124 us (21%)
  other arithmetic  23.9 us (4%)
  between operations  14.3 us (2%)
  blocking collectives  10.5 us (2%)
    dot_general x14, matrix products, local(): dot = lambda u, w: jnp.dot(u, w, preferred_element_type=f32)  209 us
    pallas_call x2, Pallas kernels, attend(): pl.pallas_call(functools.partial(attn_body, rev, npiece, nblk), grid_spec...  124 us
    all_gather x4, waiting for transfers between devices, local(): ag = lambda u: lax.all_gather(u, 'tp', axis=0, tiled=True)  113 us
    reduce_scatter x2, waiting for transfers between devices, local(): lax.psum_scatter(dot(hid, w2).astype(jnp.bfloat16), 'tp', scatter_dimensi...  40.5 us
    reduce_scatter x2, waiting for transfers between devices, local(): y = lax.psum_scatter(y, 'tp', scatter_dimension=0, tiled=True)  38.7 us
  transfers between devices with their start and end apart: 10, of which 6 were waited for; matrix products, arithmetic and copies ran while one was open for 37% of the time, Pallas kernels for 21%

profile of v1, /device:TPU:97, one launch (start us, length us, event | category | flops | bytes accessed | tf_op | source)
XLA Modules:
  0.0 584.6 jit_solution(8197060085196064091)
XLA Ops:
  6.6 1.5 fusion.9
  8.1 1.2 slice.37
  9.3 0.7 convert_element_type.127
  10.0 2.4 fusion.11
  12.5 0.3 fusion.6
  12.7 1.2 fusion.8
  14.0 0.1 all-gather.13.cloned.1.call-update
  14.0 0.1 all-gather.9.cloned.1.call-start
  14.1 0.7 all-gather.9.cloned.1.call-update
  14.8 0.1 all-gather.11.cloned.1.call-start
  14.9 10.5 %all-gather.1 = s32[4,1,256]{2,1,0:T(1,128)S(1)} all-gather(s32[1,1,256]{2,1,0:T(1,128)S(1)} %bitcast.67), channel_id=2, replica_groups=mesh['dp'=1,'tp'=4,'cp'=8] {'tp'}, dimensions={0}, use_global_device_ids=true | all-gather | bytes 5120 | tf_op jit(solution)/shard_map/all_gather | solution.py:128
  25.4 33.6 %all-gather.13.cloned.1.call-done = bf16[512,3584]{1,0:T(8,128)(2,1)} async-done(((bf16[128,3584]{1,0:T(8,128)(2,1)}), bf16[512,3584]{1,0:T(8,128)(2,1)}) %all-gather.13.cloned.1.call-update) | async-done | bytes 3670032 | tf_op jit(solution)/shard_map/all_gather | solution.py:130
  59.0 3.1 convolution_bitcast_fusion
  62.2 39.9 %all-gather.9.cloned.1.call-done = bf16[512,3584]{1,0:T(8,128)(2,1)} async-done(((bf16[128,3584]{1,0:T(8,128)(2,1)}), bf16[512,3584]{1,0:T(8,128)(2,1)}) %all-gather.9.cloned.1.call-update) | async-done | bytes 3670032 | tf_op jit(solution)/shard_map/all_gather | solution.py:130
  102.0 3.3 convolution_bitcast_fusion.1
  105.3 2.4 fusion.40
  107.7 1.1 convolution_convert_fusion.3
  108.9 0.8 pad_maximum_fusion.3
  109.7 0.1 all-gather.11.cloned.1.call-update
  109.8 0.1 all-gather.17.cloned.1.call-start
  109.9 1.0 multiply_cosine_fusion.2
  110.8 3.2 convolution_convert_fusion.2
  114.0 0.8 pad_maximum_fusion.4
  114.9 0.1 all-gather.17.cloned.1.call-update
  114.9 0.6 reduce-scatter.5.cloned.1.call-start
  115.5 7.6 %fusion.44 = f32[512,896]{0,1:T(8,128)S(1)} fusion(bf16[512,3584]{1,0:T(8,128)(2,1)} %all-gather.13.cloned.1.call-done, bf16[3584,896]{1,0:T(8,128)(2,1)} %param.15), kind=kOutput, calls=%fused_computation.88 | convolution fusion | flops 3288334336 | bytes 11927552 | tf_op jit(solution)/shard_map/dot_general | solution.py:131
  123.1 5.8 fusion.43
  128.9 0.7 subtract_convert_fusion
  129.6 0.1 pad_maximum_fusion.1
  129.6 1.3 copy.25.q_ref
  130.9 0.1 pad_maximum_fusion.2
  131.0 2.4 all-gather.11.cloned.1.call-done.refs_0_
  133.4 15.6 %attn_a.1 = bf16[512,896]{1,0:T(8,128)(2,1)} custom-call(s32[1]{0:T(128)} %bitcast.c_ref, bf16[512,896]{1,0:T(8,128)(2,1)} %copy.25.q_ref, bf16[4096,256]{1,0:T(8,128)(2,1)} %all-gather.11.cloned.1.call-done.refs_0_), custom_call_target="tpu_custom_call" | custom-call | flops 14092861440 | bytes 4849664 | tf_op jit(solution)/shard_map/attn_a/pallas_call | solution.py:105
  149.0 8.9 %convolution_convert_fusion.1 = bf16[512,3584]{1,0:T(8,128)(2,1)} fusion(bf16[512,896]{1,0:T(8,128)(2,1)} %attn_a.1, bf16[896,3584]{1,0:T(8,128)(2,1)} %param.18), kind=kOutput, calls=%fused_computation.7 | convolution fusion | flops 3290169344 | bytes 11010048 | tf_op jit(solution)/shard_map/dot_general | solution.py:131
  157.9 0.1 reduce-scatter.5.cloned.1.call-update
  157.9 0.2 reduce-scatter.9.cloned.1.call-start
  158.2 1.3 copy.29.q_ref
  159.5 108.1 %attn_b.1 = bf16[512,896]{1,0:T(8,128)(2,1)} custom-call(s32[1]{0:T(128)} %bitcast.c_ref, bf16[512,896]{1,0:T(8,128)(2,1)} %copy.29.q_ref, bf16[4096,256]{1,0:T(8,128)(2,1)} %all-gather.11.cloned.1.call-done.refs_0_, bf16[4096,256]{1,0:T(8,128)(2,1)} %all-gather.17.cloned.1.call-done.refs_1_), custom_call_target="tpu_custom_call" | custom-call | flops 36641439744 | bytes 6946816 | tf_op jit(solution)/shard_map/attn_b/pallas_call | solution.py:105
  267.5 8.9 %convolution_convert_fusion = bf16[512,3584]{1,0:T(8,128)(2,1)} fusion(bf16[512,896]{1,0:T(8,128)(2,1)} %attn_b.1, bf16[896,3584]{1,0:T(8,128)(2,1)} %param.18), kind=kOutput, calls=%fused_computation.6 | convolution fusion | flops 3290169344 | bytes 11010048 | tf_op jit(solution)/shard_map/dot_general | solution.py:131
  276.5 0.1 reduce-scatter.9.cloned.1.call-update
  276.5 0.1 all-gather.19.cloned.1.call-start
  276.6 0.6 copy-done.6
  277.2 0.8 copy-done.2
  278.0 1.6 fusion.13
  279.5 2.4 fusion.15
  282.0 38.7 %reduce-scatter.9.cloned.1.call-done = bf16[128,3584]{1,0:T(8,128)(2,1)} async-done(((bf16[512,3584]{1,0:T(8,128)(2,1)}), bf16[128,3584]{1,0:T(8,128)(2,1)}) %reduce-scatter.9.cloned.1.call-update) | async-done | bytes 917520 | tf_op jit(solution)/shard_map/reduce_scatter | solution.py:155
  320.7 1.6 fusion.17
  322.3 2.4 fusion.19
  324.7 0.1 all-gather.19.cloned.1.call-update
  324.8 0.1 all-gather.15.cloned.1.call-start
  324.9 0.7 all-gather.15.cloned.1.call-update
  325.6 0.3 reduce-scatter.11.cloned.1.call-start
  325.9 39.9 %all-gather.19.cloned.1.call-done = bf16[512,3584]{1,0:T(8,128)(2,1)} async-done(((bf16[128,3584]{1,0:T(8,128)(2,1)}), bf16[512,3584]{1,0:T(8,128)(2,1)}) %all-gather.19.cloned.1.call-update) | async-done | bytes 3670032 | tf_op jit(solution)/shard_map/all_gather | solution.py:130
  365.8 28.2 %fusion.46 = f32[512,4736]{1,0:T(8,128)} fusion(bf16[512,3584]{1,0:T(8,128)(2,1)} %all-gather.19.cloned.1.call-done, bf16[3584,4736]{1,0:T(8,128)(2,1)} %param.19), kind=kOutput, calls=%fused_computation.90 | convolution fusion | flops 17381195776 | bytes 47316992 | tf_op jit(solution)/shard_map/dot_general | solution.py:131
  393.9 27.6 %multiply_convert_fusion.clone.6 = bf16[512,4736]{1,0:T(8,128)(2,1)} fusion(f32[512,4736]{1,0:T(8,128)} %fusion.46, bf16[512,3584]{1,0:T(8,128)(2,1)S(1)} %copy-done.9, bf16[3584,4736]{1,0:T(8,128)(2,1)} %param.20), kind=kOutput, calls=%fused_computation.clone.clone.clone.clone.clone.1 | convolution fusion | flops 17395744768 | bytes 52166656 | tf_op jit(solution)/shard_map/dot_general | solution.py:131
  421.5 27.3 %fusion.2 = bf16[512,3584]{1,0:T(8,128)(2,1)} fusion(bf16[4736,3584]{1,0:T(8,128)(2,1)} %param.21, bf16[512,4736]{1,0:T(8,128)(2,1)} %multiply_convert_fusion.clone.6), kind=kOutput, calls=%fused_computation.4 | convolution fusion | flops 17383030784 | bytes 42467328 | tf_op jit(solution)/shard_map/dot_general | solution.py:131
  448.9 0.1 reduce-scatter.11.cloned.1.call-update
  448.9 0.1 reduce-scatter.7.cloned.1.call-start
  449.0 28.5 %fusion.45 = f32[512,4736]{1,0:T(8,128)} fusion(bf16[512,3584]{1,0:T(8,128)(2,1)} %all-gather.15.cloned.1.call-done, bf16[3584,4736]{1,0:T(8,128)(2,1)} %param.19), kind=kOutput, calls=%fused_computation.89 | convolution fusion | flops 17381195776 | bytes 47316992 | tf_op jit(solution)/shard_map/dot_general | solution.py:131
  477.6 27.6 %multiply_convert_fusion.1.clone.4 = bf16[512,4736]{1,0:T(8,128)(2,1)} fusion(f32[512,4736]{1,0:T(8,128)} %fusion.45, bf16[512,3584]{1,0:T(8,128)(2,1)S(1)} %copy-done.8, bf16[3584,4736]{1,0:T(8,128)(2,1)} %param.20), kind=kOutput, calls=%fused_computation.1.clone.clone.clone.clone.clone | convolution fusion | flops 17395744768 | bytes 52166656 | tf_op jit(solution)/shard_map/dot_general | solution.py:131
  505.2 27.5 %fusion.3 = bf16[512,3584]{1,0:T(8,128)(2,1)} fusion(bf16[4736,3584]{1,0:T(8,128)(2,1)} %param.21, bf16[512,4736]{1,0:T(8,128)(2,1)} %multiply_convert_fusion.1.clone.4), kind=kOutput, calls=%fused_computation.5 | convolution fusion | flops 17383030784 | bytes 42467328 | tf_op jit(solution)/shard_map/dot_general | solution.py:131
  532.7 0.1 reduce-scatter.7.cloned.1.call-update
  532.8 40.5 %reduce-scatter.7.cloned.1.call-done = bf16[128,3584]{1,0:T(8,128)(2,1)} async-done(((bf16[512,3584]{1,0:T(8,128)(2,1)}), bf16[128,3584]{1,0:T(8,128)(2,1)}) %reduce-scatter.7.cloned.1.call-update) | async-done | bytes 917520 | tf_op jit(solution)/shard_map/reduce_scatter | solution.py:162
  573.3 3.9 fusion.16
  (33 shorter events, 0.1 us)
Async XLA Ops:
  6.5 52.4 %copy-start = (bf16[3584,128]{1,0:T(8,128)(2,1)S(1)}, bf16[3584,128]{1,0:T(8,128)(2,1)}, u32[]{:S(2)}) copy-start(bf16[3584,128]{1,0:T(8,128)(2,1)} %param.16) | copy-start | bytes 2752516
  6.6 52.4 %all-gather.13.cloned.1.call-start = ((), (), s32[]{:S(2)}) async-start(), calls=%async_computation.6 | async-start | bytes 4587520 | tf_op jit(solution)/shard_map/all_gather | solution.py:130
  9.3 5.6 copy-start.7
  14.0 88.0 %all-gather.9.cloned.1.call-start = ((), (), s32[]{:S(2)}) async-start(), calls=%async_computation.4 | async-start | bytes 4587520 | tf_op jit(solution)/shard_map/all_gather | solution.py:130
  14.8 118.5 %all-gather.11.cloned.1.call-start = ((), (), s32[]{:S(2)}) async-start(), calls=%async_computation.5 | async-start | bytes 2359296 | tf_op jit(solution)/shard_map/all_gather | solution.py:143
  62.1 45.6 %copy-start.10 = (bf16[3584,128]{1,0:T(8,128)(2,1)S(1)}, bf16[3584,128]{1,0:T(8,128)(2,1)}, u32[]{:S(2)}) copy-start(bf16[3584,128]{1,0:T(8,128)(2,1)} %param.17) | copy-start | bytes 2752516
  102.0 5.7 copy-start.4
  109.8 49.7 %all-gather.17.cloned.1.call-start = ((), (), s32[]{:S(2)}) async-start(), calls=%async_computation.10 | async-start | bytes 2359296 | tf_op jit(solution)/shard_map/all_gather | solution.py:143
  114.9 162.2 %reduce-scatter.5.cloned.1.call-start = ((), (), s32[]{:S(2)}) async-start(), calls=%async_computation.7 | async-start | bytes 4587520 | tf_op jit(solution)/shard_map/reduce_scatter | solution.py:155
  115.5 7.6 %copy-start.5 = (bf16[512,3584]{1,0:T(8,128)(2,1)S(1)}, bf16[512,3584]{1,0:T(8,128)(2,1)}, u32[]{:S(2)}) copy-start(bf16[512,3584]{1,0:T(8,128)(2,1)} %all-gather.9.cloned.1.call-done) | copy-start | bytes 11010052
  157.9 162.8 %reduce-scatter.9.cloned.1.call-start = ((), (), s32[]{:S(2)}) async-start(), calls=%async_computation.11 | async-start | bytes 4587520 | tf_op jit(solution)/shard_map/reduce_scatter | solution.py:155
  276.5 0.7 copy-start.6
  276.5 1.5 copy-start.2
  276.5 89.2 %all-gather.19.cloned.1.call-start = ((), (), s32[]{:S(2)}) async-start(), calls=%async_computation.12 | async-start | bytes 4587520 | tf_op jit(solution)/shard_map/all_gather | solution.py:130
  324.8 124.2 %all-gather.15.cloned.1.call-start = ((), (), s32[]{:S(2)}) async-start(), calls=%async_computation.8 | async-start | bytes 4587520 | tf_op jit(solution)/shard_map/all_gather | solution.py:130
  325.6 207.2 %reduce-scatter.11.cloned.1.call-start = ((), (), s32[]{:S(2)}) async-start(), calls=%async_computation.13 | async-start | bytes 4587520 | tf_op jit(solution)/shard_map/reduce_scatter | solution.py:162
  365.8 28.2 %copy-start.9 = (bf16[512,3584]{1,0:T(8,128)(2,1)S(1)}, bf16[512,3584]{1,0:T(8,128)(2,1)}, u32[]{:S(2)}) copy-start(bf16[512,3584]{1,0:T(8,128)(2,1)} %all-gather.19.cloned.1.call-done) | copy-start | bytes 11010052
  448.9 124.3 %reduce-scatter.7.cloned.1.call-start = ((), (), s32[]{:S(2)}) async-start(), calls=%async_computation.9 | async-start | bytes 4587520 | tf_op jit(solution)/shard_map/reduce_scatter | solution.py:162
  449.0 28.6 %copy-start.8 = (bf16[512,3584]{1,0:T(8,128)(2,1)S(1)}, bf16[512,3584]{1,0:T(8,128)(2,1)}, u32[]{:S(2)}) copy-start(bf16[512,3584]{1,0:T(8,128)(2,1)} %all-gather.15.cloned.1.call-done) | copy-start | bytes 11010052
  532.7 40.6 %copy-start.3 = (bf16[256,3584]{1,0:T(8,128)(2,1)S(1)}, bf16[256,3584]{1,0:T(8,128)(2,1)}, u32[]{:S(2)}) copy-start(bf16[256,3584]{1,0:T(8,128)(2,1)} %param.11) | copy-start | bytes 5505028
  532.7 44.4 %copy-start.1 = (bf16[3584,128]{1,0:T(8,128)(2,1)S(1)}, bf16[3584,128]{1,0:T(8,128)(2,1)}, u32[]{:S(2)}) copy-start(bf16[3584,128]{1,0:T(8,128)(2,1)} %param.16) | copy-start | bytes 2752516
Sparse Core Ops, SparseCore 0:
  14.1 44.8 all-gather.12
  60.6 41.4 all-gather.8
  109.9 23.4 all-gather.10
  134.8 23.1 all-gather.16
  160.2 77.6 reduce-scatter.4
  276.6 44.0 reduce-scatter.8
  324.9 40.7 all-gather.18
  367.3 41.4 all-gather.14
  449.1 40.3 reduce-scatter.10
  532.9 40.3 reduce-scatter.6

commit v2 on v0

v2 whole, which is shorter than its diff:
```python
import functools
import math
import jax
import jax.numpy as jnp
from jax import lax
from jax.experimental import pallas as pl
from jax.experimental.pallas import tpu as pltpu
from jax.sharding import PartitionSpec as P

DH = 128
EPS = 1e-5
THETA = 500000.0
NEG = -1e30
PAIR = 2


def rms_norm(v, g):
    vf = v.astype(jnp.float32)
    inv = lax.rsqrt(jnp.mean(vf * vf, axis=-1, keepdims=True) + EPS)
    return (vf * inv * g.astype(jnp.float32)).astype(jnp.bfloat16)


def rope_tables(p):
    freq = 1.0 / (THETA ** (jnp.arange(0, DH, 2, dtype=jnp.float32) / DH))
    ang = p.astype(jnp.float32)[:, None] * freq
    c, s = jnp.cos(ang), jnp.sin(ang)
    return jnp.concatenate([c, c], axis=1), jnp.concatenate([-s, s], axis=1)


def proj_body(roped, a_ref, w_ref, c_ref, s_ref, o_ref):
    nb, piece, d = a_ref.shape
    y = jnp.dot(a_ref[...].reshape(nb * piece, d), w_ref[...], preferred_element_type=jnp.float32)
    for t in range(y.shape[1] // DH):
        yt = y[:, t * DH:(t + 1) * DH]
        if t < roped:
            yt = yt * c_ref[...] + pltpu.roll(yt, DH // 2, 1) * s_ref[...]
        o_ref[:, t * DH:(t + 1) * DH] = yt.astype(o_ref.dtype)


def proj(a, i, w, c, s, roped, tn):
    nb, _, piece, d = a.shape
    n = nb * piece
    wd = w.shape[1]
    return pl.pallas_call(
        functools.partial(proj_body, roped),
        grid=(pl.cdiv(wd, tn),),
        in_specs=[
            pl.BlockSpec((nb, None, piece, d), lambda t: (0, i, 0, 0)),
            pl.BlockSpec((d, tn), lambda t: (0, t)),
            pl.BlockSpec((n, DH), lambda t: (0, 0)),
            pl.BlockSpec((n, DH), lambda t: (0, 0)),
        ],
        out_specs=pl.BlockSpec((n, tn), lambda t: (0, t)),
        out_shape=jax.ShapeDtypeStruct((n, wd), jnp.bfloat16),
        compiler_params=pltpu.CompilerParams(dimension_semantics=("arbitrary",)),
        cost_estimate=pl.CostEstimate(flops=2 * n * d * wd, bytes_accessed=2 * (n * d + d * wd + n * wd), transcendentals=0),
    )(a, w, c, s)


def mm_body(x_ref, w_ref, o_ref):
    o_ref[...] = jnp.dot(x_ref[...], w_ref[...], preferred_element_type=jnp.float32).astype(o_ref.dtype)


def mm(x, w, tn):
    n, d = x.shape
    wd = w.shape[1]
    return pl.pallas_call(
        mm_body,
        grid=(pl.cdiv(wd, tn),),
        in_specs=[pl.BlockSpec((n, d), lambda t: (0, 0)), pl.BlockSpec((d, tn), lambda t: (0, t))],
        out_specs=pl.BlockSpec((n, tn), lambda t: (0, t)),
        out_shape=jax.ShapeDtypeStruct((n, wd), jnp.bfloat16),
        compiler_params=pltpu.CompilerParams(dimension_semantics=("arbitrary",)),
        cost_estimate=pl.CostEstimate(flops=2 * n * d * wd, bytes_accessed=2 * (n * d + d * wd + n * wd), transcendentals=0),
    )(x, w)


def gate_body(b_ref, w1_ref, w3_ref, o_ref):
    n = b_ref.shape[0]
    step = n // 2
    for r in range(0, n, step):
        b = b_ref[r:r + step, :]
        g = jnp.dot(b, w1_ref[...], preferred_element_type=jnp.float32)
        u = jnp.dot(b, w3_ref[...], preferred_element_type=jnp.float32)
        o_ref[r:r + step, :] = (jax.nn.silu(g) * u).astype(o_ref.dtype)


def gate_up(b, w1, w3, tn):
    n, d = b.shape
    wd = w1.shape[1]
    return pl.pallas_call(
        gate_body,
        grid=(pl.cdiv(wd, tn),),
        in_specs=[pl.BlockSpec((n, d), lambda t: (0, 0)), pl.BlockSpec((d, tn), lambda t: (0, t)), pl.BlockSpec((d, tn), lambda t: (0, t))],
        out_specs=pl.BlockSpec((n, tn), lambda t: (0, t)),
        out_shape=jax.ShapeDtypeStruct((n, wd), jnp.bfloat16),
        compiler_params=pltpu.CompilerParams(dimension_semantics=("arbitrary",)),
        cost_estimate=pl.CostEstimate(flops=4 * n * d * wd, bytes_accessed=2 * (n * d + 2 * d * wd + n * wd), transcendentals=n * wd),
        name="gate_up",
    )(b, w1, w3)


def attn_body(rev, npiece, nblk, c_ref, q_ref, *refs):
    if rev:
        kva_ref, kvb_ref, o_ref, kv_s, kt_s, q_s, acc, m_s, l_s, sem = refs
    else:
        kva_ref, o_ref, kv_s, kt_s, q_s, acc, m_s, l_s, sem = refs
    c = c_ref[0]
    g = pl.program_id(0)
    piece, w = q_ref.shape
    heads = w // DH
    n = piece * npiece
    rows_all = heads * piece
    na = nblk * n
    coef = math.log2(math.e) / math.sqrt(DH)
    nt = n // DH

    @pl.when(g == 0)
    def _():
        cps = [pltpu.make_async_copy(kva_ref, kv_s.at[pl.ds(0, na)], sem.at[0])]
        if rev:
            cps.append(pltpu.make_async_copy(kvb_ref, kv_s.at[pl.ds(na, na)], sem.at[1]))
        for cp in cps:
            cp.start()
        for cp in cps:
            cp.wait()

        @pl.loop(0, kt_s.shape[0])
        def _(i):
            k = kv_s[pl.ds(pl.multiple_of(i * n, n), n), :DH]
            kt_s[i] = k.T

    for h in range(heads):
        q_s[h * piece:(h + 1) * piece, :] = q_ref[:, h * DH:(h + 1) * DH]

    def step(blocks, diag, first):
        kvs = [(kt_s[i], kv_s[pl.ds(pl.multiple_of(i * n, n), n), DH:]) for i in blocks]
        for r0 in (0,):
            rows = pl.ds(r0, rows_all)
            q = q_s[rows, :]
            tiles = []
            for k, _ in kvs:
                s = jnp.dot(q, k, preferred_element_type=jnp.float32)
                if diag:
                    r = lax.broadcasted_iota(jnp.int32, s.shape, 0) % piece
                    t = lax.broadcasted_iota(jnp.int32, s.shape, 1)
                    u = t // piece
                    ahead = (u < g) if rev else (u > g)
                    keep = jnp.logical_and(jnp.logical_not(ahead), jnp.logical_or(u != g, t % piece <= r))
                    s = jnp.where(keep, s, NEG)
                tiles.append([s[:, u * DH:(u + 1) * DH] for u in range(nt)])
            flat = [t for ts in tiles for t in ts]
            mx = functools.reduce(jnp.maximum, flat)
            mx = jnp.max(mx, axis=1, keepdims=True)
            if first:
                m = jnp.broadcast_to(mx, (rows_all, DH))
            else:
                m0 = m_s[rows, :]
                m = jnp.maximum(m0, mx)
            part = None
            pv = None
            for ts, (_, v) in zip(tiles, kvs):
                ps = [jnp.exp2((t - m) * coef) for t in ts]
                for p in ps:
                    part = p if part is None else part + p
                pb = jnp.concatenate([p.astype(jnp.bfloat16) for p in ps], axis=1)
                d = jnp.dot(pb, v, preferred_element_type=jnp.float32)
                pv = d if pv is None else pv + d
            if first:
                l_s[rows, :] = part
                acc[rows, :] = pv
            else:
                al = jnp.exp2((m0 - m) * coef)
                l_s[rows, :] = l_s[rows, :] * al + part
                acc[rows, :] = acc[rows, :] * al + pv
            m_s[rows, :] = m

    step([c + nblk if rev else c], True, True)
    count = (2 * nblk - 1 - c) if rev else c
    idx = (lambda t: jnp.where(t < nblk, t, t + c + 1)) if rev else (lambda t: t)

    @pl.loop(0, count // PAIR)
    def _(t):
        step([idx(PAIR * t + u) for u in range(PAIR)], False, False)

    if PAIR > 1:
        @pl.loop(count // PAIR * PAIR, count)
        def _(t):
            step([idx(t)], False, False)
    for h in range(heads):
        rows = slice(h * piece, (h + 1) * piece)
        l = jnp.sum(l_s[rows, :], axis=1, keepdims=True)
        o_ref[:, h * DH:(h + 1) * DH] = (acc[rows, :] / l).astype(o_ref.dtype)


def attend(rev, npiece, nblk, c, q, *kvs):
    n, w = q.shape[0] // 2, q.shape[1]
    piece = n // npiece
    off = npiece if rev else 0
    heads = w // DH
    units = (nblk + 1 + nblk // 2) if rev else nblk // 2 + 1
    blocks = len(kvs) * nblk
    gs = pltpu.PrefetchScalarGridSpec(
        num_scalar_prefetch=1,
        grid=(npiece,),
        in_specs=[pl.BlockSpec((piece, w), lambda g, c: (g + off, 0))]
        + [pl.BlockSpec(memory_space=pl.ANY) for kv in kvs],
        out_specs=pl.BlockSpec((piece, w), lambda g, c: (g, 0)),
        scratch_shapes=[
            pltpu.VMEM((blocks * n, 2 * DH), jnp.bfloat16),
            pltpu.VMEM((blocks, DH, n), jnp.bfloat16),
            pltpu.VMEM((heads * piece, DH), jnp.bfloat16),
        ] + [pltpu.VMEM((heads * piece, DH), jnp.float32)] * 3 + [pltpu.SemaphoreType.DMA((2,))],
    )
    return pl.pallas_call(
        functools.partial(attn_body, rev, npiece, nblk),
        grid_spec=gs,
        out_shape=jax.ShapeDtypeStruct((n, w), jnp.bfloat16),
        compiler_params=pltpu.CompilerParams(dimension_semantics=("arbitrary",)),
        cost_estimate=pl.CostEstimate(
            flops=units * heads * n * n * DH * 4 * 3, bytes_accessed=3 * n * w * 2 + sum(kv.size * 2 for kv in kvs),
            transcendentals=units * heads * n * n),
        name="attn_b" if rev else "attn_a",
    )(c, q, *kvs)


def solution(mesh):
    tok = P(('dp', 'cp', 'tp'), None)
    col = P(None, 'tp')
    row = P('tp', None)
    ntp = mesh.shape['tp']
    ncp = mesh.shape['cp']

    def local(x, pos, g1, g2, wq, wk, wv, wo, w1, w3, w2):
        f32 = jnp.float32
        half = x.shape[0] // 2
        xs = [x[:half], x[half:]]
        bar = lax.optimization_barrier
        cidx = lax.axis_index('cp').astype(jnp.int32).reshape(1)
        ag = lambda u: lax.all_gather(u, 'tp', axis=0, tiled=True)
        rs = lambda u: lax.psum_scatter(u, 'tp', scatter_dimension=0, tiled=True)

        a = ag(rms_norm(x, g1)).reshape(ntp, 2, half, -1)
        pg = lax.all_gather(pos, 'tp', axis=0).reshape(ntp, 2, half)
        wkv = jnp.concatenate([wk, wv], axis=1)
        tabs = [rope_tables(pg[:, i].reshape(-1)) for i in range(2)]
        kvs = [proj(a, i, wkv, *tabs[i], 1, 2 * DH) for i in range(2)]
        kvg = [lax.all_gather(kv, 'cp', axis=0, tiled=True) for kv in kvs]
        qs = jnp.concatenate([proj(a, i, wq, *tabs[i], 2, 2 * DH) for i in range(2)], axis=0)

        oa = attend(False, ntp, ncp, cidx, qs, kvg[0])
        ya = mm(oa, wo, 512)
        ya, qs = bar((ya, qs))
        yb = mm(attend(True, ntp, ncp, cidx, qs, *kvg), wo, 512)
        h0 = (xs[0].astype(f32) + rs(ya).astype(f32)).astype(jnp.bfloat16)
        b0 = rms_norm(h0, g2)
        yb, b0 = bar((yb, b0))
        b0 = ag(b0)
        yb = rs(yb)
        m0, yb = bar((gate_up(b0, w1, w3, 2 * DH), yb))
        h1 = (xs[1].astype(f32) + yb.astype(f32)).astype(jnp.bfloat16)
        b1 = rms_norm(h1, g2)
        m0, b1 = bar((m0, b1))
        z0 = mm(m0, w2, 2 * DH)
        z1 = mm(gate_up(ag(b1), w1, w3, 2 * DH), w2, 2 * DH)
        outs = []
        for h, z in ((h0, z0), (h1, z1)):
            z = rs(z)
            outs.append((h.astype(f32) + z.astype(f32)).astype(jnp.bfloat16))
        return jnp.concatenate(outs, axis=0)

    return jax.shard_map(local, mesh=mesh, in_specs=(tok, P(('dp', 'cp', 'tp')), P(None), P(None), col, col, col, row, col, col, row), out_specs=tok, check_vma=False)
```

time: 984 us -> 457 us (0.46)
  matrix products: 389 us -> 0 us
  Pallas kernels: 0 us -> 247 us
  waiting for transfers between devices: 400 us -> 159 us
  other arithmetic: 133 us -> 20.5 us
  blocking collectives: 29.7 us -> 10.4 us
    dot_general x23 -> x0, matrix products: 389 us -> none  [the longest x8 110 us: blk(): o = jnp.einsum('kgqs,skd->qkgd', w, v, preferred_element_type=jnp.float32)]
    pallas_call x0 -> x12, Pallas kernels: none -> 247 us  [the longest x2 89.7 us: gate_up(): pl.pallas_call(gate_body, grid=(pl.cdiv(wd, tn),), in_specs=[pl.BlockSpec...]
    reduce_scatter x2 -> x4, waiting for transfers between devices: 258 us -> 40.6 us  [local(): rs = lambda u: lax.psum_scatter(u, 'tp', scatter_dimension=0, tiled=True)]
    reduce_sum x8 -> x0, other arithmetic: 110 us -> none  [blk(): w = (e / jnp.sum(e, axis=-1, keepdims=True)).astype(jnp.bfloat16)]
    all_gather x4 -> x5, waiting for transfers between devices: 141 us -> 118 us  [the longest x3 116 us: local(): ag = lambda u: lax.all_gather(u, 'tp', axis=0, tiled=True)]
    all_gather x2 -> x1, blocking collectives: 29.7 us -> 10.4 us  [local(): pg = lax.all_gather(pos, 'tp', axis=0).reshape(ntp, 2, half)]
  transfers between devices with their start and end apart: 6 -> 9, of which waited for: 5 -> 5; matrix products, arithmetic and copies ran while one was open for 3% -> 2% of each run, Pallas kernels for 0% -> 53%
where the time goes in v2:
time: 457 us; the launch traced here: 455 us
  Pallas kernels  247 us (54%)
  waiting for transfers between devices  159 us (35%)
  other arithmetic  20.5 us (4%)
  between operations  13.3 us (3%)
  blocking collectives  10.4 us (2%)
    all_gather x3, waiting for transfers between devices, local(): ag = lambda u: lax.all_gather(u, 'tp', axis=0, tiled=True)  116 us
    pallas_call x2, Pallas kernels, gate_up(): pl.pallas_call(gate_body, grid=(pl.cdiv(wd, tn),), in_specs=[pl.BlockSpec...  89.7 us
    pallas_call x4, Pallas kernels, mm(): pl.pallas_call(mm_body, grid=(pl.cdiv(wd, tn),), in_specs=[pl.BlockSpec((...  72.2 us
    pallas_call x2, Pallas kernels, attend(): pl.pallas_call(functools.partial(attn_body, rev, npiece, nblk), grid_spec...  58.8 us
    reduce_scatter x4, waiting for transfers between devices, local(): rs = lambda u: lax.psum_scatter(u, 'tp', scatter_dimension=0, tiled=True)  40.6 us
    pallas_call x4, Pallas kernels, proj(): pl.pallas_call(functools.partial(proj_body, roped), grid=(pl.cdiv(wd, tn)...  26.6 us
    all_gather x1, blocking collectives, local(): pg = lax.all_gather(pos, 'tp', axis=0).reshape(ntp, 2, half)  10.4 us
  transfers between devices with their start and end apart: 9, of which 5 were waited for; matrix products, arithmetic and copies ran while one was open for 2% of the time, Pallas kernels for 53%

profile of v2, /device:TPU:97, one launch (start us, length us, event | category | flops | bytes accessed | tf_op | source)
XLA Modules:
  0.0 454.6 jit_solution(5846215978716706848)
XLA Ops:
  6.5 0.0 copy-start
  6.5 0.0 all-gather.8.cloned.1.call-start
  6.6 2.1 fusion
  8.6 0.7 convert_element_type.79
  9.3 0.0 copy-done
  9.3 1.7 fusion.2
  11.1 0.0 copy-start.7
  11.1 0.1 all-gather.8.cloned.1.call-update
  11.2 0.0 copy-start.4
  11.2 0.1 all-gather.10.cloned.1.call-start
  11.2 0.5 copy-done.7
  11.8 10.4 %all-gather.1 = s32[4,1,256]{2,1,0:T(1,128)S(1)} all-gather(s32[1,1,256]{2,1,0:T(1,128)S(1)} %bitcast.13), channel_id=2, replica_groups=mesh['dp'=1,'tp'=4,'cp'=8] {'tp'}, dimensions={0}, use_global_device_ids=true | all-gather | bytes 5120 | tf_op jit(solution)/shard_map/all_gather | solution.py:244
  22.2 1.9 fusion.11
  24.1 0.0 copy-start.5
  24.1 1.0 pad_maximum_fusion.2
  25.2 0.0 copy-done.4
  25.2 1.1 constant_dynamic-update-slice_fusion.1
  26.3 0.0 copy-done.5
  26.3 1.0 constant_dynamic-update-slice_fusion.w_ref
  27.3 59.6 %all-gather.8.cloned.1.call-done = bf16[1024,3584]{1,0:T(8,128)(2,1)} async-done(((bf16[256,3584]{1,0:T(8,128)(2,1)}), bf16[1024,3584]{1,0:T(8,128)(2,1)}) %all-gather.8.cloned.1.call-update) | async-done | bytes 7340048 | tf_op jit(solution)/shard_map/all_gather | solution.py:240
  86.9 4.5 %shard_map.111 = bf16[512,256]{1,0:T(8,128)(2,1)} custom-call(bf16[4,2,128,3584]{3,2,1,0:T(8,128)(2,1)} %bitcast.6, bf16[3584,256]{1,0:T(8,128)(2,1)} %constant_dynamic-update-slice_fusion.w_ref, f32[512,128]{1,0:T(8,128)} %get-tuple-element.34.c_ref, f32[512,128]{1,0:T(8,128)} %get-tuple-element.35.s_ref), custom_call_target="tpu_custom_call" | custom-call | flops 939524096 | bytes 5767168 | tf_op jit(solution)/shard_map/pallas_call | solution.py:44
  91.5 0.1 all-gather.10.cloned.1.call-update
  91.5 0.1 all-gather.12.cloned.1.call-start
  91.6 1.0 pad_maximum_fusion.4
  92.6 4.6 %shard_map.113 = bf16[512,256]{1,0:T(8,128)(2,1)} custom-call(bf16[4,2,128,3584]{3,2,1,0:T(8,128)(2,1)} %bitcast.7, bf16[3584,256]{1,0:T(8,128)(2,1)} %constant_dynamic-update-slice_fusion.w_ref, f32[512,128]{1,0:T(8,128)} %get-tuple-element.36.c_ref, f32[512,128]{1,0:T(8,128)} %get-tuple-element.37.s_ref), custom_call_target="tpu_custom_call" | custom-call | flops 939524096 | bytes 5767168 | tf_op jit(solution)/shard_map/pallas_call | solution.py:44
  97.2 0.1 all-gather.12.cloned.1.call-update
  97.2 0.1 reduce-scatter.5.cloned.1.call-start
  97.3 8.7 %shard_map.110 = bf16[512,896]{1,0:T(8,128)(2,1)} custom-call(bf16[4,2,128,3584]{3,2,1,0:T(8,128)(2,1)} %bitcast.8, bf16[3584,896]{1,0:T(8,128)(2,1)} %w_ref.7, f32[512,128]{1,0:T(8,128)} %get-tuple-element.36.c_ref, f32[512,128]{1,0:T(8,128)} %get-tuple-element.37.s_ref), custom_call_target="tpu_custom_call" | custom-call | flops 3288334336 | bytes 11010048 | tf_op jit(solution)/shard_map/pallas_call | solution.py:44
  106.0 8.8 %shard_map.109 = bf16[512,896]{1,0:T(8,128)(2,1)} custom-call(bf16[4,2,128,3584]{3,2,1,0:T(8,128)(2,1)} %bitcast.9, bf16[3584,896]{1,0:T(8,128)(2,1)} %w_ref.7, f32[512,128]{1,0:T(8,128)} %get-tuple-element.34.c_ref, f32[512,128]{1,0:T(8,128)} %get-tuple-element.35.s_ref), custom_call_target="tpu_custom_call" | custom-call | flops 3288334336 | bytes 11010048 | tf_op jit(solution)/shard_map/pallas_call | solution.py:44
  114.8 0.0 copy-done.3
  114.8 2.6 pad_maximum_fusion.q_ref
  117.4 0.0 all-gather.10.cloned.1.call-done.refs_0_
  117.4 11.6 %attn_a.1.x_ref = bf16[512,896]{1,0:T(8,128)(2,1)} custom-call(s32[1]{0:T(128)} %bitcast.c_ref, bf16[1024,896]{1,0:T(8,128)(2,1)} %pad_maximum_fusion.q_ref, bf16[4096,256]{1,0:T(8,128)(2,1)} %all-gather.10.cloned.1.call-done.refs_0_), custom_call_target="tpu_custom_call" | custom-call | flops 14092861440 | bytes 4849664 | tf_op jit(solution)/shard_map/attn_a/pallas_call | solution.py:215
  128.9 9.4 %shard_map.112 = bf16[512,3584]{1,0:T(8,128)(2,1)} custom-call(bf16[512,896]{1,0:T(8,128)(2,1)} %attn_a.1.x_ref, bf16[896,3584]{1,0:T(8,128)(2,1)} %w_ref.9), custom_call_target="tpu_custom_call" | custom-call | flops 3288334336 | bytes 11010048 | tf_op jit(solution)/shard_map/pallas_call | solution.py:67
  138.3 0.1 reduce-scatter.5.cloned.1.call-update
  138.4 0.2 all-gather.14.cloned.1.call-start
  138.6 0.4 copy-done.6
  139.0 1.4 all-gather.12.cloned.1.call-done.refs_1_
  140.5 47.3 %attn_b.1.x_ref = bf16[512,896]{1,0:T(8,128)(2,1)} custom-call(s32[1]{0:T(128)} %bitcast.c_ref, bf16[1024,896]{1,0:T(8,128)(2,1)} %pad_maximum_fusion.q_ref, bf16[4096,256]{1,0:T(8,128)(2,1)} %all-gather.10.cloned.1.call-done.refs_0_, bf16[4096,256]{1,0:T(8,128)(2,1)} %all-gather.12.cloned.1.call-done.refs_1_), custom_call_target="tpu_custom_call" | custom-call | flops 36641439744 | bytes 6946816 | tf_op jit(solution)/shard_map/attn_b/pallas_call | solution.py:215
  187.8 9.3 %shard_map.114 = bf16[512,3584]{1,0:T(8,128)(2,1)} custom-call(bf16[512,896]{1,0:T(8,128)(2,1)} %attn_b.1.x_ref, bf16[896,3584]{1,0:T(8,128)(2,1)} %w_ref.9), custom_call_target="tpu_custom_call" | custom-call | flops 3288334336 | bytes 11010048 | tf_op jit(solution)/shard_map/pallas_call | solution.py:67
  197.1 1.6 fusion.3
  198.7 0.0 copy-done.1
  198.8 1.3 fusion.5
  200.0 0.1 all-gather.14.cloned.1.call-update
  200.1 0.1 reduce-scatter.7.cloned.1.call-start
  200.1 0.6 reduce-scatter.7.cloned.1.call-update
  200.7 0.1 all-gather.16.cloned.1.call-start
  200.8 42.2 %all-gather.14.cloned.1.call-done.b_ref = bf16[512,3584]{1,0:T(8,128)(2,1)} async-done(((bf16[128,3584]{1,0:T(8,128)(2,1)}), bf16[512,3584]{1,0:T(8,128)(2,1)}) %all-gather.14.cloned.1.call-update) | async-done | bytes 3670032 | tf_op jit(solution)/shard_map/all_gather | solution.py:240
  243.0 45.0 %gate_up.2.x_ref = bf16[512,4736]{1,0:T(8,128)(2,1)} custom-call(bf16[512,3584]{1,0:T(8,128)(2,1)} %all-gather.14.cloned.1.call-done.b_ref, bf16[3584,4736]{1,0:T(8,128)(2,1)} %w1_ref.3, bf16[3584,4736]{1,0:T(8,128)(2,1)} %w3_ref.3), custom_call_target="tpu_custom_call" | custom-call | flops 34762391552 | bytes 76414976 | tf_op jit(solution)/shard_map/gate_up/pallas_call | solution.py:91
  288.0 1.6 fusion.7
  289.6 0.0 copy-done.2
  289.6 1.3 fusion.9
  290.9 0.1 all-gather.16.cloned.1.call-update
  291.0 0.1 reduce-scatter.9.cloned.1.call-start
  291.0 26.9 %shard_map.115 = bf16[512,3584]{1,0:T(8,128)(2,1)} custom-call(bf16[512,4736]{1,0:T(8,128)(2,1)} %gate_up.2.x_ref, bf16[4736,3584]{1,0:T(8,128)(2,1)} %w_ref.11), custom_call_target="tpu_custom_call" | custom-call | flops 17381195776 | bytes 42467328 | tf_op jit(solution)/shard_map/pallas_call | solution.py:67
  317.9 0.1 reduce-scatter.9.cloned.1.call-update
  318.0 0.1 reduce-scatter.11.cloned.1.call-start
  318.0 14.4 %all-gather.16.cloned.1.call-done.b_ref = bf16[512,3584]{1,0:T(8,128)(2,1)} async-done(((bf16[128,3584]{1,0:T(8,128)(2,1)}), bf16[512,3584]{1,0:T(8,128)(2,1)}) %all-gather.16.cloned.1.call-update) | async-done | bytes 3670032 | tf_op jit(solution)/shard_map/all_gather | solution.py:240
  332.5 44.8 %gate_up.3.x_ref = bf16[512,4736]{1,0:T(8,128)(2,1)} custom-call(bf16[512,3584]{1,0:T(8,128)(2,1)} %all-gather.16.cloned.1.call-done.b_ref, bf16[3584,4736]{1,0:T(8,128)(2,1)} %w1_ref.3, bf16[3584,4736]{1,0:T(8,128)(2,1)} %w3_ref.3), custom_call_target="tpu_custom_call" | custom-call | flops 34762391552 | bytes 76414976 | tf_op jit(solution)/shard_map/gate_up/pallas_call | solution.py:91
  377.2 26.6 %shard_map.116 = bf16[512,3584]{1,0:T(8,128)(2,1)} custom-call(bf16[512,4736]{1,0:T(8,128)(2,1)} %gate_up.3.x_ref, bf16[4736,3584]{1,0:T(8,128)(2,1)} %w_ref.11), custom_call_target="tpu_custom_call" | custom-call | flops 17381195776 | bytes 42467328 | tf_op jit(solution)/shard_map/pallas_call | solution.py:67
  403.8 0.1 reduce-scatter.11.cloned.1.call-update
  403.9 0.0 reduce-scatter.9.cloned.1.call-done
  403.9 40.6 %reduce-scatter.11.cloned.1.call-done = bf16[128,3584]{1,0:T(8,128)(2,1)} async-done(((bf16[512,3584]{1,0:T(8,128)(2,1)}), bf16[128,3584]{1,0:T(8,128)(2,1)}) %reduce-scatter.11.cloned.1.call-update) | async-done | bytes 917520 | tf_op jit(solution)/shard_map/reduce_scatter | solution.py:241
  444.5 3.6 fusion.6
  (13 shorter events, 0.1 us)
Async XLA Ops:
  6.5 2.8 copy-start
  6.5 80.4 %all-gather.8.cloned.1.call-start = ((), (), s32[]{:S(2)}) async-start(), calls=%async_computation.4 | async-start | bytes 9175040 | tf_op jit(solution)/shard_map/all_gather | solution.py:240
  11.1 0.7 copy-start.7
  11.2 14.0 %copy-start.4 = (bf16[3584,128]{1,0:T(8,128)(2,1)S(1)}, bf16[3584,128]{1,0:T(8,128)(2,1)}, u32[]{:S(2)}) copy-start(bf16[3584,128]{1,0:T(8,128)(2,1)} %param.16) | copy-start | bytes 2752516
  11.2 106.2 %all-gather.10.cloned.1.call-start = ((), (), s32[]{:S(2)}) async-start(), calls=%async_computation.5 | async-start | bytes 2359296 | tf_op jit(solution)/shard_map/all_gather | solution.py:248
  24.1 2.2 copy-start.5
  91.5 48.9 %all-gather.12.cloned.1.call-start = ((), (), s32[]{:S(2)}) async-start(), calls=%async_computation.7 | async-start | bytes 2359296 | tf_op jit(solution)/shard_map/all_gather | solution.py:248
  97.2 99.9 %reduce-scatter.5.cloned.1.call-start = ((), (), s32[]{:S(2)}) async-start(), calls=%async_computation.6 | async-start | bytes 4587520 | tf_op jit(solution)/shard_map/reduce_scatter | solution.py:241
  106.0 8.8 %copy-start.3 = (bf16[512,896]{1,0:T(8,128)(2,1)S(1)}, bf16[512,896]{1,0:T(8,128)(2,1)}, u32[]{:S(2)}) copy-start(bf16[512,896]{1,0:T(8,128)(2,1)} %shard_map.110) | copy-start | bytes 2752516
  138.3 0.7 copy-start.6
  138.4 104.6 %all-gather.14.cloned.1.call-start = ((), (), s32[]{:S(2)}) async-start(), calls=%async_computation.8 | async-start | bytes 4587520 | tf_op jit(solution)/shard_map/all_gather | solution.py:240
  197.1 1.6 copy-start.1
  200.1 87.9 %reduce-scatter.7.cloned.1.call-start = ((), (), s32[]{:S(2)}) async-start(), calls=%async_computation.9 | async-start | bytes 4587520 | tf_op jit(solution)/shard_map/reduce_scatter | solution.py:241
  200.7 131.8 %all-gather.16.cloned.1.call-start = ((), (), s32[]{:S(2)}) async-start(), calls=%async_computation.11 | async-start | bytes 4587520 | tf_op jit(solution)/shard_map/all_gather | solution.py:240
  288.0 1.6 copy-start.2
  291.0 112.9 %reduce-scatter.9.cloned.1.call-start = ((), (), s32[]{:S(2)}) async-start(), calls=%async_computation.10 | async-start | bytes 4587520 | tf_op jit(solution)/shard_map/reduce_scatter | solution.py:241
  318.0 126.5 %reduce-scatter.11.cloned.1.call-start = ((), (), s32[]{:S(2)}) async-start(), calls=%async_computation.12 | async-start | bytes 4587520 | tf_op jit(solution)/shard_map/reduce_scatter | solution.py:241
Sparse Core Ops, SparseCore 0:
  11.3 75.6 all-gather.7
  91.7 24.0 all-gather.9
  117.4 23.0 all-gather.11
  142.6 51.6 reduce-scatter.4
  200.2 42.7 all-gather.13
  245.2 40.3 reduce-scatter.6
  291.1 41.3 all-gather.15
  334.8 40.4 reduce-scatter.8
  404.0 40.4 reduce-scatter.10

commit v3 on v2

--- a/solution.py
+++ b/solution.py
@@ -73,6 +73,121 @@
         compiler_params=pltpu.CompilerParams(dimension_semantics=("arbitrary",)),
         cost_estimate=pl.CostEstimate(flops=2 * n * d * wd, bytes_accessed=2 * (n * d + d * wd + n * wd), transcendentals=0),
     )(x, w)
+
+
+def down_scatter_body(ntp, m_ref, w_ref, h_ref, o_ref, z_s, far_in, fwd, near_in, far_send, far_recv, fwd_send, fwd_recv):
+    t = pl.program_id(0)
+    last = pl.num_programs(0) - 1
+    me = lax.axis_index("tp")
+    side = (lax.rem(me + 1, ntp), lax.rem(me + ntp - 1, ntp))
+    far = lax.rem(me + 2, ntp)
+    tn = w_ref.shape[1]
+    piece = h_ref.shape[0]
+    half = piece // 2
+
+    def cols(u):
+        return pl.ds(pl.multiple_of(u * tn, tn), tn)
+
+    def rows(owner, off, size):
+        return pl.ds(pl.multiple_of(owner * piece + off, half), size)
+
+    def far_copy(d, u):
+        return pltpu.make_async_remote_copy(
+            src_ref=z_s.at[rows(far, d * half, half), cols(u)], dst_ref=far_in.at[d, :, cols(u)],
+            send_sem=far_send.at[d], recv_sem=far_recv.at[d, u],
+            device_id={"tp": side[d]}, device_id_type=pl.DeviceIdType.MESH)
+
+    def fwd_copy(d, u):
+        return pltpu.make_async_remote_copy(
+            src_ref=fwd.at[d, :, cols(u)], dst_ref=near_in.at[d, :, cols(u)],
+            send_sem=fwd_send.at[d], recv_sem=fwd_recv.at[d],
+            device_id={"tp": side[d]}, device_id_type=pl.DeviceIdType.MESH)
+
+    def send_far(u):
+        for d in range(2):
+            far_copy(d, u).start()
+
+    def send_fwd(u):
+        for d in range(2):
+            fwd_copy(d, u).start()
+
+    def add(u):
+        for d in range(2):
+            far_copy(d, u).wait_recv()
+            mine = slice(d * half, (d + 1) * half)
+            rest = slice((1 - d) * half, (2 - d) * half)
+            got = far_in[d, :, cols(u)].astype(jnp.float32)
+            own = z_s[rows(side[d], d * half, half), cols(u)].astype(jnp.float32)
+            fwd[d, mine, cols(u)] = (own + got).astype(fwd.dtype)
+            fwd[d, rest, cols(u)] = z_s[rows(side[d], (1 - d) * half, half), cols(u)]
+
+    @pl.when(t == 0)
+    def _():
+        bar = pltpu.get_barrier_semaphore()
+        for d in range(2):
+            pl.semaphore_signal(bar, inc=1, device_id={"tp": side[d]}, device_id_type=pl.DeviceIdType.MESH)
+        pl.semaphore_wait(bar, 2)
+
+    z_s[:, cols(t)] = jnp.dot(m_ref[...], w_ref[...], preferred_element_type=jnp.float32).astype(z_s.dtype)
+
+    @pl.when(t >= 1)
+    def _():
+        send_far(t - 1)
+
+    @pl.when(t >= 3)
+    def _():
+        add(t - 3)
+
+    @pl.when(t >= 4)
+    def _():
+        send_fwd(t - 4)
+
+    @pl.when(t == last)
+    def _():
+        send_far(last)
+        send_fwd(last - 3)
+
+        @pl.loop(last - 2, last + 1)
+        def _(u):
+            add(u)
+            send_fwd(u)
+
+        for d in range(2):
+            whole = pltpu.make_async_remote_copy(
+                src_ref=fwd.at[d], dst_ref=near_in.at[d], send_sem=fwd_send.at[d], recv_sem=fwd_recv.at[d],
+                device_id={"tp": side[d]}, device_id_type=pl.DeviceIdType.MESH)
+            whole.wait()
+            pltpu.make_async_remote_copy(
+                src_ref=far_in.at[d], dst_ref=far_in.at[d], send_sem=far_send.at[d], recv_sem=far_recv.at[d, 0],
+                device_id={"tp": side[d]}, device_id_type=pl.DeviceIdType.MESH).wait_send()
+
+        @pl.loop(0, last + 1)
+        def _(u):
+            own = z_s[rows(me, 0, piece), cols(u)].astype(jnp.float32)
+            z = own + near_in[0, :, cols(u)].astype(jnp.float32) + near_in[1, :, cols(u)].astype(jnp.float32)
+            o_ref[:, cols(u)] = (h_ref[:, cols(u)].astype(jnp.float32) + z).astype(o_ref.dtype)
+
+
+def down_scatter(ntp, m, w, h, tn):
+    n, d = m.shape
+    wd = w.shape[1]
+    piece = n // ntp
+    tiles = wd // tn
+    bf = jnp.bfloat16
+    return pl.pallas_call(
+        functools.partial(down_scatter_body, ntp),
+        grid=(tiles,),
+        in_specs=[pl.BlockSpec((n, d), lambda t: (0, 0)), pl.BlockSpec((d, tn), lambda t: (0, t)), pl.BlockSpec((piece, wd), lambda t: (0, 0))],
+        out_specs=pl.BlockSpec((piece, wd), lambda t: (0, 0)),
+        out_shape=jax.ShapeDtypeStruct((piece, wd), bf),
+        scratch_shapes=[
+            pltpu.VMEM((n, wd), bf), pltpu.VMEM((2, piece // 2, wd), bf), pltpu.VMEM((2, piece, wd), bf), pltpu.VMEM((2, piece, wd), bf),
+            pltpu.SemaphoreType.DMA((2,)), pltpu.SemaphoreType.DMA((2, tiles)), pltpu.SemaphoreType.DMA((2,)), pltpu.SemaphoreType.DMA((2,)),
+        ],
+        compiler_params=pltpu.CompilerParams(dimension_semantics=("arbitrary",), collective_id=0, has_side_effects=True),
+        cost_estimate=pl.CostEstimate(flops=2 * n * d * wd, bytes_accessed=2 * (n * d + d * wd + n * wd), transcendentals=0),
+        name="down_scatter",
+    )(m, w, h)
 
 
 def gate_body(b_ref, w1_ref, w3_ref, o_ref):
@@ -249,9 +364,9 @@
         qs = jnp.concatenate([proj(a, i, wq, *tabs[i], 2, 2 * DH) for i in range(2)], axis=0)
 
         oa = attend(False, ntp, ncp, cidx, qs, kvg[0])
-        ya = mm(oa, wo, 512)
+        ya = mm(oa, wo, wo.shape[1] // 2)
         ya, qs = bar((ya, qs))
-        yb = mm(attend(True, ntp, ncp, cidx, qs, *kvg), wo, 512)
+        yb = mm(attend(True, ntp, ncp, cidx, qs, *kvg), wo, wo.shape[1] // 2)
         h0 = (xs[0].astype(f32) + rs(ya).astype(f32)).astype(jnp.bfloat16)
         b0 = rms_norm(h0, g2)
         yb, b0 = bar((yb, b0))
@@ -262,11 +377,9 @@
         b1 = rms_norm(h1, g2)
         m0, b1 = bar((m0, b1))
         z0 = mm(m0, w2, 2 * DH)
-        z1 = mm(gate_up(ag(b1), w1, w3, 2 * DH), w2, 2 * DH)
-        outs = []
-        for h, z in ((h0, z0), (h1, z1)):
-            z = rs(z)
-            outs.append((h.astype(f32) + z.astype(f32)).astype(jnp.bfloat16))
-        return jnp.concatenate(outs, axis=0)
+        m1 = gate_up(ag(b1), w1, w3, 2 * DH)
+        out0 = (h0.astype(f32) + rs(z0).astype(f32)).astype(jnp.bfloat16)
+        out1 = down_scatter(ntp, m1, w2, h1, 2 * DH)
+        return jnp.concatenate([out0, out1], axis=0)
 
     return jax.shard_map(local, mesh=mesh, in_specs=(tok, P(('dp', 'cp', 'tp')), P(None), P(None), col, col, col, row, col, col, row), out_specs=tok, check_vma=False)

time: 457 us -> 431 us (0.943)
  waiting for transfers between devices: 159 us -> 120 us
  Pallas kernels: 247 us -> 261 us
    pallas_call x0 -> x1, Pallas kernels: none -> 43.9 us  [down_scatter(): pl.pallas_call(functools.partial(down_scatter_body, ntp), grid=(tiles,),...]
    reduce_scatter x4 -> x3, waiting for transfers between devices: 40.6 us -> 0.02 us  [local(): rs = lambda u: lax.psum_scatter(u, 'tp', scatter_dimension=0, tiled=True)]
    pallas_call x4 -> x3, Pallas kernels: 72.2 us -> 42.2 us  [mm(): pl.pallas_call(mm_body, grid=(pl.cdiv(wd, tn),), in_specs=[pl.BlockSpec((...]
  transfers between devices with their start and end apart: 9 -> 8, of which waited for: 5 -> 4; matrix products, arithmetic and copies ran while one was open for 2% -> 2% of each run, Pallas kernels for 53% -> 60%
where the time goes in v3:
time: 431 us; the launch traced here: 430 us
  Pallas kernels  261 us (61%)
  waiting for transfers between devices  120 us (28%)
  other arithmetic  19.7 us (5%)
  between operations  13.6 us (3%)
  blocking collectives  10.4 us (2%)
    all_gather x3, waiting for transfers between devices, local(): ag = lambda u: lax.all_gather(u, 'tp', axis=0, tiled=True)  116 us
    pallas_call x2, Pallas kernels, gate_up(): pl.pallas_call(gate_body, grid=(pl.cdiv(wd, tn),), in_specs=[pl.BlockSpec...  89.7 us
    pallas_call x2, Pallas kernels, attend(): pl.pallas_call(functools.partial(attn_body, rev, npiece, nblk), grid_spec...  58.8 us
    pallas_call x1, Pallas kernels, down_scatter(): pl.pallas_call(functools.partial(down_scatter_body, ntp), grid=(tiles,),...  43.9 us
    pallas_call x3, Pallas kernels, mm(): pl.pallas_call(mm_body, grid=(pl.cdiv(wd, tn),), in_specs=[pl.BlockSpec((...  42.2 us
    pallas_call x4, Pallas kernels, proj(): pl.pallas_call(functools.partial(proj_body, roped), grid=(pl.cdiv(wd, tn)...  26.7 us
    all_gather x1, blocking collectives, local(): pg = lax.all_gather(pos, 'tp', axis=0).reshape(ntp, 2, half)  10.4 us
  transfers between devices with their start and end apart: 8, of which 4 were waited for; matrix products, arithmetic and copies ran while one was open for 2% of the time, Pallas kernels for 60%

profile of v3, /device:TPU:97, one launch (start us, length us, event | category | flops | bytes accessed | tf_op | source)
XLA Modules:
  0.0 430.1 jit_solution(15932017009153676464)
XLA Ops:
  6.5 0.0 copy-start
  6.5 0.0 all-gather.8.cloned.1.call-start
  6.6 2.1 fusion
  8.6 0.7 convert_element_type.72
  9.3 0.0 copy-done
  9.3 1.7 fusion.2
  11.1 0.0 copy-start.8
  11.1 0.1 all-gather.8.cloned.1.call-update
  11.2 0.0 copy-start.5
  11.2 0.1 all-gather.10.cloned.1.call-start
  11.2 0.5 copy-done.8
  11.8 10.4 %all-gather.1 = s32[4,1,256]{2,1,0:T(1,128)S(1)} all-gather(s32[1,1,256]{2,1,0:T(1,128)S(1)} %bitcast.13), channel_id=2, replica_groups=mesh['dp'=1,'tp'=4,'cp'=8] {'tp'}, dimensions={0}, use_global_device_ids=true | all-gather | bytes 5120 | tf_op jit(solution)/shard_map/all_gather | solution.py:359
  22.2 1.9 fusion.10
  24.1 0.0 copy-start.6
  24.1 1.0 pad_maximum_fusion.2
  25.2 0.0 copy-done.5
  25.2 1.1 constant_dynamic-update-slice_fusion.1
  26.3 0.0 copy-done.6
  26.3 1.0 constant_dynamic-update-slice_fusion.w_ref
  27.3 59.6 %all-gather.8.cloned.1.call-done = bf16[1024,3584]{1,0:T(8,128)(2,1)} async-done(((bf16[256,3584]{1,0:T(8,128)(2,1)}), bf16[1024,3584]{1,0:T(8,128)(2,1)}) %all-gather.8.cloned.1.call-update) | async-done | bytes 7340048 | tf_op jit(solution)/shard_map/all_gather | solution.py:355
  86.9 4.5 %shard_map.111 = bf16[512,256]{1,0:T(8,128)(2,1)} custom-call(bf16[4,2,128,3584]{3,2,1,0:T(8,128)(2,1)} %bitcast.6, bf16[3584,256]{1,0:T(8,128)(2,1)} %constant_dynamic-update-slice_fusion.w_ref, f32[512,128]{1,0:T(8,128)} %get-tuple-element.34.c_ref, f32[512,128]{1,0:T(8,128)} %get-tuple-element.35.s_ref), custom_call_target="tpu_custom_call" | custom-call | flops 939524096 | bytes 5767168 | tf_op jit(solution)/shard_map/pallas_call | solution.py:44
  91.5 0.1 all-gather.10.cloned.1.call-update
  91.5 0.1 all-gather.12.cloned.1.call-start
  91.6 1.0 pad_maximum_fusion.4
  92.6 4.6 %shard_map.113 = bf16[512,256]{1,0:T(8,128)(2,1)} custom-call(bf16[4,2,128,3584]{3,2,1,0:T(8,128)(2,1)} %bitcast.7, bf16[3584,256]{1,0:T(8,128)(2,1)} %constant_dynamic-update-slice_fusion.w_ref, f32[512,128]{1,0:T(8,128)} %get-tuple-element.36.c_ref, f32[512,128]{1,0:T(8,128)} %get-tuple-element.37.s_ref), custom_call_target="tpu_custom_call" | custom-call | flops 939524096 | bytes 5767168 | tf_op jit(solution)/shard_map/pallas_call | solution.py:44
  97.2 0.1 all-gather.12.cloned.1.call-update
  97.2 0.2 reduce-scatter.4.cloned.1.call-start
  97.5 8.7 %shard_map.110 = bf16[512,896]{1,0:T(8,128)(2,1)} custom-call(bf16[4,2,128,3584]{3,2,1,0:T(8,128)(2,1)} %bitcast.8, bf16[3584,896]{1,0:T(8,128)(2,1)} %w_ref.7, f32[512,128]{1,0:T(8,128)} %get-tuple-element.36.c_ref, f32[512,128]{1,0:T(8,128)} %get-tuple-element.37.s_ref), custom_call_target="tpu_custom_call" | custom-call | flops 3288334336 | bytes 11010048 | tf_op jit(solution)/shard_map/pallas_call | solution.py:44
  106.2 8.8 %shard_map.109 = bf16[512,896]{1,0:T(8,128)(2,1)} custom-call(bf16[4,2,128,3584]{3,2,1,0:T(8,128)(2,1)} %bitcast.9, bf16[3584,896]{1,0:T(8,128)(2,1)} %w_ref.7, f32[512,128]{1,0:T(8,128)} %get-tuple-element.34.c_ref, f32[512,128]{1,0:T(8,128)} %get-tuple-element.35.s_ref), custom_call_target="tpu_custom_call" | custom-call | flops 3288334336 | bytes 11010048 | tf_op jit(solution)/shard_map/pallas_call | solution.py:44
  115.1 0.0 copy-done.3
  115.1 2.6 pad_maximum_fusion.q_ref
  117.6 11.6 %attn_a.1.x_ref = bf16[512,896]{1,0:T(8,128)(2,1)} custom-call(s32[1]{0:T(128)} %bitcast.c_ref, bf16[1024,896]{1,0:T(8,128)(2,1)} %pad_maximum_fusion.q_ref, bf16[4096,256]{1,0:T(8,128)(2,1)} %all-gather.10.cloned.1.call-done.refs_0_), custom_call_target="tpu_custom_call" | custom-call | flops 14092861440 | bytes 4849664 | tf_op jit(solution)/shard_map/attn_a/pallas_call | solution.py:330
  129.2 7.7 %shard_map.112 = bf16[512,3584]{1,0:T(8,128)(2,1)} custom-call(bf16[512,896]{1,0:T(8,128)(2,1)} %attn_a.1.x_ref, bf16[896,3584]{1,0:T(8,128)(2,1)} %w_ref.9), custom_call_target="tpu_custom_call" | custom-call | flops 3288334336 | bytes 11010048 | tf_op jit(solution)/shard_map/pallas_call | solution.py:67
  136.9 0.1 reduce-scatter.4.cloned.1.call-update
  137.0 0.1 all-gather.14.cloned.1.call-start
  137.1 0.6 copy-done.7
  137.6 2.8 all-gather.12.cloned.1.call-done.refs_1_
  140.5 47.3 %attn_b.1.x_ref = bf16[512,896]{1,0:T(8,128)(2,1)} custom-call(s32[1]{0:T(128)} %bitcast.c_ref, bf16[1024,896]{1,0:T(8,128)(2,1)} %pad_maximum_fusion.q_ref, bf16[4096,256]{1,0:T(8,128)(2,1)} %all-gather.10.cloned.1.call-done.refs_0_, bf16[4096,256]{1,0:T(8,128)(2,1)} %all-gather.12.cloned.1.call-done.refs_1_), custom_call_target="tpu_custom_call" | custom-call | flops 36641439744 | bytes 6946816 | tf_op jit(solution)/shard_map/attn_b/pallas_call | solution.py:330
  187.8 7.6 %shard_map.114 = bf16[512,3584]{1,0:T(8,128)(2,1)} custom-call(bf16[512,896]{1,0:T(8,128)(2,1)} %attn_b.1.x_ref, bf16[896,3584]{1,0:T(8,128)(2,1)} %w_ref.9), custom_call_target="tpu_custom_call" | custom-call | flops 3288334336 | bytes 11010048 | tf_op jit(solution)/shard_map/pallas_call | solution.py:67
  195.3 1.6 fusion.6
  197.0 0.0 copy-done.1
  197.0 1.3 fusion.8
  198.2 0.1 all-gather.14.cloned.1.call-update
  198.3 0.1 reduce-scatter.6.cloned.1.call-start
  198.4 0.6 reduce-scatter.6.cloned.1.call-update
  198.9 0.3 all-gather.16.cloned.1.call-start
  199.2 42.1 %all-gather.14.cloned.1.call-done.b_ref = bf16[512,3584]{1,0:T(8,128)(2,1)} async-done(((bf16[128,3584]{1,0:T(8,128)(2,1)}), bf16[512,3584]{1,0:T(8,128)(2,1)}) %all-gather.14.cloned.1.call-update) | async-done | bytes 3670032 | tf_op jit(solution)/shard_map/all_gather | solution.py:355
  241.3 45.0 %gate_up.2.x_ref = bf16[512,4736]{1,0:T(8,128)(2,1)} custom-call(bf16[512,3584]{1,0:T(8,128)(2,1)} %all-gather.14.cloned.1.call-done.b_ref, bf16[3584,4736]{1,0:T(8,128)(2,1)} %w1_ref.3, bf16[3584,4736]{1,0:T(8,128)(2,1)} %w3_ref.3), custom_call_target="tpu_custom_call" | custom-call | flops 34762391552 | bytes 76414976 | tf_op jit(solution)/shard_map/gate_up/pallas_call | solution.py:206
  286.3 1.6 fusion.3
  287.9 0.0 copy-start.2
  287.9 1.0 copy-done.2
  288.8 1.2 fusion.5
  290.0 0.1 all-gather.16.cloned.1.call-update
  290.1 0.1 reduce-scatter.8.cloned.1.call-start
  290.2 26.9 %shard_map.115 = bf16[512,3584]{1,0:T(8,128)(2,1)} custom-call(bf16[512,4736]{1,0:T(8,128)(2,1)} %gate_up.2.x_ref, bf16[4736,3584]{1,0:T(8,128)(2,1)} %w_ref.11), custom_call_target="tpu_custom_call" | custom-call | flops 17381195776 | bytes 42467328 | tf_op jit(solution)/shard_map/pallas_call | solution.py:67
  317.0 0.1 reduce-scatter.8.cloned.1.call-update
  317.1 14.5 %all-gather.16.cloned.1.call-done.b_ref = bf16[512,3584]{1,0:T(8,128)(2,1)} async-done(((bf16[128,3584]{1,0:T(8,128)(2,1)}), bf16[512,3584]{1,0:T(8,128)(2,1)}) %all-gather.16.cloned.1.call-update) | async-done | bytes 3670032 | tf_op jit(solution)/shard_map/all_gather | solution.py:355
  331.6 44.7 %gate_up.3.m_ref = bf16[512,4736]{1,0:T(8,128)(2,1)} custom-call(bf16[512,3584]{1,0:T(8,128)(2,1)} %all-gather.16.cloned.1.call-done.b_ref, bf16[3584,4736]{1,0:T(8,128)(2,1)} %w1_ref.3, bf16[3584,4736]{1,0:T(8,128)(2,1)} %w3_ref.3), custom_call_target="tpu_custom_call" | custom-call | flops 34762391552 | bytes 76414976 | tf_op jit(solution)/shard_map/gate_up/pallas_call | solution.py:206
  376.3 43.9 %down_scatter.1 = bf16[128,3584]{1,0:T(8,128)(2,1)} custom-call(bf16[512,4736]{1,0:T(8,128)(2,1)} %gate_up.3.m_ref, bf16[4736,3584]{1,0:T(8,128)(2,1)} %w_ref.11, bf16[128,3584]{1,0:T(8,128)(2,1)} %copy-done.2), custom_call_target="tpu_custom_call" | custom-call | flops 17381195776 | bytes 42467328 | tf_op jit(solution)/shard_map/down_scatter/pallas_call | solution.py:177
  420.2 0.0 reduce-scatter.8.cloned.1.call-done
  420.3 0.0 copy-start.4
  420.3 1.6 fusion.9
  421.9 0.0 copy-done.4
  421.9 1.3 pad_maximum_fusion.1
  (12 shorter events, 0.1 us)
Async XLA Ops:
  6.5 2.8 copy-start
  6.5 80.4 %all-gather.8.cloned.1.call-start = ((), (), s32[]{:S(2)}) async-start(), calls=%async_computation.3 | async-start | bytes 9175040 | tf_op jit(solution)/shard_map/all_gather | solution.py:355
  11.1 0.7 copy-start.8
  11.2 14.0 %copy-start.5 = (bf16[3584,128]{1,0:T(8,128)(2,1)S(1)}, bf16[3584,128]{1,0:T(8,128)(2,1)}, u32[]{:S(2)}) copy-start(bf16[3584,128]{1,0:T(8,128)(2,1)} %param.16) | copy-start | bytes 2752516
  11.2 106.5 %all-gather.10.cloned.1.call-start = ((), (), s32[]{:S(2)}) async-start(), calls=%async_computation.4 | async-start | bytes 2359296 | tf_op jit(solution)/shard_map/all_gather | solution.py:363
  24.1 2.2 copy-start.6
  91.5 48.9 %all-gather.12.cloned.1.call-start = ((), (), s32[]{:S(2)}) async-start(), calls=%async_computation.6 | async-start | bytes 2359296 | tf_op jit(solution)/shard_map/all_gather | solution.py:363
  97.2 98.1 %reduce-scatter.4.cloned.1.call-start = ((), (), s32[]{:S(2)}) async-start(), calls=%async_computation.5 | async-start | bytes 4587520 | tf_op jit(solution)/shard_map/reduce_scatter | solution.py:356
  106.2 8.8 %copy-start.3 = (bf16[512,896]{1,0:T(8,128)(2,1)S(1)}, bf16[512,896]{1,0:T(8,128)(2,1)}, u32[]{:S(2)}) copy-start(bf16[512,896]{1,0:T(8,128)(2,1)} %shard_map.110) | copy-start | bytes 2752516
  136.9 0.7 copy-start.7
  137.0 104.3 %all-gather.14.cloned.1.call-start = ((), (), s32[]{:S(2)}) async-start(), calls=%async_computation.7 | async-start | bytes 4587520 | tf_op jit(solution)/shard_map/all_gather | solution.py:355
  195.3 1.6 copy-start.1
  198.3 88.0 %reduce-scatter.6.cloned.1.call-start = ((), (), s32[]{:S(2)}) async-start(), calls=%async_computation.8 | async-start | bytes 4587520 | tf_op jit(solution)/shard_map/reduce_scatter | solution.py:356
  198.9 132.7 %all-gather.16.cloned.1.call-start = ((), (), s32[]{:S(2)}) async-start(), calls=%async_computation.10 | async-start | bytes 4587520 | tf_op jit(solution)/shard_map/all_gather | solution.py:355
  287.9 1.0 copy-start.2
  290.1 130.1 %reduce-scatter.8.cloned.1.call-start = ((), (), s32[]{:S(2)}) async-start(), calls=%async_computation.9 | async-start | bytes 4587520 | tf_op jit(solution)/shard_map/reduce_scatter | solution.py:356
  420.3 1.6 copy-start.4
Sparse Core Ops, SparseCore 0:
  11.3 75.6 all-gather.7
  91.7 24.0 all-gather.9
  117.4 23.0 all-gather.11
  142.6 50.2 reduce-scatter.3
  198.4 42.8 all-gather.13
  243.5 40.3 reduce-scatter.5
  290.2 41.3 all-gather.15
  333.9 40.4 reduce-scatter.7
